TPU v7x, 256 devices: a whole 4x4x8 slice. The times are simulated.
256 devices in a mesh: cp: 32 (over z_hi, x, core), tp: 8 (over z_lo, y).
Axes of the slice: x: 4, y: 4, z: 8 (z_hi: 4, z_lo: 2; z = z_hi * 2 + z_lo), core: 2. Of those that a mesh axis runs over, the one named last changes fastest.
Arguments:
- hidden: bfloat16 [16384, 4096], P('cp', 'tp'), may hold values from -6 to 6
- norm_gain: float32 [4096], replicated, may hold values from 0.5 to 1.5
- w_query: bfloat16 [4096, 4096], P(None, 'tp'), may hold values from -0.140625 to 0.140625
- w_key: bfloat16 [4096, 1024], P(None, 'tp'), may hold values from -4 to 4
- w_value: bfloat16 [4096, 1024], P(None, 'tp'), may hold values from -0.09375 to 0.09375
- w_out: bfloat16 [4096, 4096], P('tp'), may hold values from -0.5 to 0.5
- doc_ids: int32 [16384], P('cp'), may hold values from 0 to 5, never falling along the last dimension, each value on 1 to 12288 neighbouring positions
Outputs:
- updated: bfloat16 [16384, 4096], P('cp', 'tp')
Inputs may be any that keep to these rules, and one draw needn't show every extreme that they name: `doc_ids`: document numbers never fall along the sequence; every document has 1 to 12288 tokens.
All inputs are finite; a program needn't handle non-finite values.
Results may differ from a plain program's by a relative error of at most 0.017.
The roundings to bfloat16 on the way count: a program that leaves them out, or rounds other values in their place, can miss the bound.
Values may be sent and summed in bfloat16 or wider, within the bound.
A program may use at most 128 MiB of HBM per device.

v0:
```python
import jax
import jax.numpy as jnp
from jax import lax
from jax.sharding import PartitionSpec as P

HEADS = 32
KV_HEADS = 8
HEAD_SIZE = 128


epsilon = 1e-05
rope_base = 500000.0


def from_everyone(shard, axis):
    copies = jnp.broadcast_to(shard, (lax.axis_size(axis), *shard.shape))
    return lax.all_to_all(copies, axis, split_axis=0, concat_axis=0, tiled=True)


def taken_together(shard, axis):
    return from_everyone(shard, axis).sum(axis=0)


def in_one_piece(arrays, axis, dim, along):
    columns = [a.reshape(*a.shape[:along], -1) for a in arrays]
    both = jnp.concatenate(columns, axis=along)
    out, at, done = (lax.all_gather(both, axis, axis=dim, tiled=True), 0, [])
    for a, column in zip(arrays, columns):
        share = out[..., at : at + column.shape[along]]
        done.append(share.reshape(*share.shape[:along], *a.shape[along:]))
        at += column.shape[along]
    return tuple(done)


def split_up(shard, dim, length):
    lengths = shard.shape
    tiles = shard.reshape(*lengths[:dim], length, lengths[dim] // length, *lengths[dim + 1 :])
    return jnp.moveaxis(tiles, dim, 0)


def sum_at_owner(shard, axis, dim):
    tiles = split_up(shard, dim, lax.axis_size(axis))
    arrived = lax.all_to_all(tiles, axis, split_axis=0, concat_axis=0, tiled=True)
    return arrived.astype(jnp.float32).sum(axis=0)


def rotate(vectors, positions):
    half = HEAD_SIZE // 2
    freqs = rope_base ** (-jnp.arange(half, dtype=jnp.float32) * 2.0 / HEAD_SIZE)
    angles = positions.astype(jnp.float32)[:, None] * freqs[None, :]
    cosine = jnp.cos(angles)[:, None, :]
    sine = jnp.sin(angles)[:, None, :]
    first = vectors[..., :half]
    second = vectors[..., half:]
    return jnp.concatenate(
        [first * cosine - second * sine, second * cosine + first * sine], axis=-1
    )


def attend_block(
    loop_state, query_matrix, query_pos, query_doc, key_matrix, value_matrix, key_pos, key_doc
):
    best, total, running_output = loop_state
    logit_matrix = jnp.einsum(
        "ucpm,ycm->cpuy", query_matrix, key_matrix, preferred_element_type=jnp.float32
    ) * HEAD_SIZE ** (-0.5)
    allowed = (key_pos[None, :] <= query_pos[:, None]) & (key_doc[None, :] == query_doc[:, None])
    masked = jnp.where(allowed, logit_matrix, jnp.float32(-1e30))
    new_best = jnp.maximum(best, jnp.max(masked, axis=-1))
    correction_scale = jnp.exp(best - new_best)
    attention_weights = jnp.where(
        allowed, jnp.exp(logit_matrix - new_best[..., None]), jnp.float32(0.0)
    )
    total = total * correction_scale + jnp.sum(attention_weights, axis=-1)
    running_output = running_output * correction_scale[..., None] + jnp.einsum(
        "sfec,csh->sfeh",
        attention_weights.astype(jnp.bfloat16),
        value_matrix,
        preferred_element_type=jnp.float32,
    )
    return (new_best, total, running_output)


def shards(hidden, norm_gain, w_query, w_key, w_value, w_out, doc_ids):
    tok_rows = hidden.shape[0]
    half_rows = tok_rows // 2
    width = norm_gain.shape[0]
    group = HEADS // KV_HEADS
    local_kv = w_key.shape[1] // HEAD_SIZE
    query_cols = w_query.shape[1]
    key_cols = w_key.shape[1]
    wide_local = hidden.astype(jnp.float32)
    squares = taken_together(jnp.sum(wide_local * wide_local, axis=1), "tp")
    inverse_rms = lax.rsqrt(squares / width + epsilon)[:, None]
    piece = lax.all_gather(hidden, "tp", axis=1, tiled=True)
    normed_piece = (piece.astype(jnp.float32) * inverse_rms * norm_gain[None, :]).astype(
        jnp.bfloat16
    )
    projected = jnp.concatenate(
        [
            jnp.dot(normed_piece, w_query, preferred_element_type=jnp.float32),
            jnp.dot(normed_piece, w_key, preferred_element_type=jnp.float32),
            jnp.dot(normed_piece, w_value, preferred_element_type=jnp.float32),
        ],
        axis=1,
    )
    cp_rank = lax.axis_index("cp")
    positions = cp_rank * tok_rows + jnp.arange(tok_rows, dtype=jnp.int32)
    query_raw = projected[:, :query_cols].reshape(tok_rows, local_kv * group, HEAD_SIZE)
    key_raw = projected[:, query_cols : query_cols + key_cols].reshape(
        tok_rows, local_kv, HEAD_SIZE
    )
    query_matrix = (
        rotate(query_raw, positions)
        .astype(jnp.bfloat16)
        .reshape(tok_rows, local_kv, group, HEAD_SIZE)
    )
    keys_flat = rotate(key_raw, positions).astype(jnp.bfloat16).reshape(tok_rows, key_cols)
    values_flat = projected[:, query_cols + key_cols :].astype(jnp.bfloat16)
    query_doc = doc_ids.astype(jnp.float32)
    docs_flat = query_doc.astype(jnp.bfloat16)
    first_queries = query_matrix[:half_rows]
    first_pos = positions[:half_rows]
    first_doc = query_doc[:half_rows]
    second_queries = query_matrix[half_rows:]
    second_doc = query_doc[half_rows:]
    second_start = cp_rank * tok_rows + half_rows
    second_pos = second_start + jnp.arange(half_rows, dtype=jnp.int32)
    last_first = cp_rank * tok_rows + half_rows - 1
    last_second = second_start + half_rows - 1
    init_half = (
        jnp.full((local_kv, group, half_rows), -1e30, jnp.float32),
        jnp.zeros((local_kv, group, half_rows), jnp.float32),
        jnp.zeros((local_kv, group, half_rows, HEAD_SIZE), jnp.float32),
    )
    init = (init_half, init_half)
    key_piece, value_piece, doc_piece = in_one_piece(
        (keys_flat, values_flat, docs_flat), "cp", 0, 1
    )
    count = key_piece.shape[0]

    def inner(index, state):
        first_state, second_state = state
        offset = index * tok_rows
        key_blk = lax.dynamic_slice_in_dim(key_piece, offset, tok_rows, 0).reshape(
            tok_rows, local_kv, HEAD_SIZE
        )
        value_blk = lax.dynamic_slice_in_dim(value_piece, offset, tok_rows, 0).reshape(
            tok_rows, local_kv, HEAD_SIZE
        )
        key_doc = lax.dynamic_slice_in_dim(doc_piece, offset, tok_rows, 0).astype(jnp.float32)
        key_pos = offset + jnp.arange(tok_rows, dtype=jnp.int32)

        def attend_first(inner_state):
            return attend_block(
                inner_state,
                first_queries,
                first_pos,
                first_doc,
                key_blk,
                value_blk,
                key_pos,
                key_doc,
            )

        def attend_second(inner_state):
            return attend_block(
                inner_state,
                second_queries,
                second_pos,
                second_doc,
                key_blk,
                value_blk,
                key_pos,
                key_doc,
            )

        first_state = lax.cond(
            offset <= last_first, attend_first, lambda inner_state: inner_state, first_state
        )
        second_state = lax.cond(
            offset <= last_second, attend_second, lambda inner_state: inner_state, second_state
        )
        return (first_state, second_state)

    final = lax.fori_loop(0, count // tok_rows, inner, init)

    def finish(state):
        result = state[2] / state[1][..., None]
        return (
            jnp.transpose(result, (2, 0, 1, 3)).reshape(half_rows, query_cols).astype(jnp.bfloat16)
        )

    attended_first = finish(final[0])
    attended_second = finish(final[1])
    attended = jnp.concatenate([attended_first, attended_second], axis=0)
    terms = jnp.dot(attended, w_out, preferred_element_type=jnp.float32)
    summed = sum_at_owner(terms.astype(jnp.bfloat16), "tp", 1)
    return summed.astype(jnp.bfloat16)


def solution(mesh):
    in_specs = (
        P("cp", "tp"),
        P(),
        P(None, "tp"),
        P(None, "tp"),
        P(None, "tp"),
        P("tp", None),
        P("cp"),
    )
    out_specs = P("cp", "tp")
    return jax.shard_map(shards, mesh=mesh, in_specs=in_specs, out_specs=out_specs, check_vma=False)
```

profile of v0, /device:TPU:199, one launch (start us, length us, event | category | flops | bytes accessed | tf_op | source)
XLA Modules:
  0.0 402.5 jit_solution(15677815882340103085)
XLA Ops:
  9.1 4.6 %all-to-all-start = ((f32[8,1,512]{2,1,0:T(1,128)}), f32[8,1,512]{2,1,0:T(1,128)S(1)}, u32[]{:S(2)}, u32[]{:S(2)}) async-start(f32[8,1,512]{2,1,0:T(1,128)} %broadcast_in_dim.61), calls=%async_computation | async-start | bytes 32768 | tf_op jit(solution)/shard_map/all_to_all | solution.py:17
  14.5 4.3 %all-to-all-done = f32[8,1,512]{2,1,0:T(1,128)S(1)} async-done(((f32[8,1,512]{2,1,0:T(1,128)}), f32[8,1,512]{2,1,0:T(1,128)S(1)}, u32[]{:S(2)}, u32[]{:S(2)}) %all-to-all-start) | async-done | bytes 16416 | tf_op jit(solution)/shard_map/all_to_all | solution.py:17
  18.9 45.1 %all-gather.3.cloned.1.call-done = bf16[512,4096]{1,0:T(8,128)(2,1)} async-done(((bf16[512,512]{1,0:T(8,128)(2,1)}), bf16[512,4096]{1,0:T(8,128)(2,1)}) %all-gather.3.cloned.1.call-update) | async-done | bytes 4194320 | tf_op jit(solution)/shard_map/all_gather | solution.py:95
  64.0 3.9 convolution_bitcast_fusion.2
  72.9 5.9 %fusion.58 = f32[512,512]{0,1:T(8,128)S(1)} fusion(bf16[4096,512]{1,0:T(8,128)(2,1)} %param.15, bf16[512,4096]{1,0:T(8,128)(2,1)} %all-gather.3.cloned.1.call-done, f32[4096]{0:T(1024)S(1)} %copy-done.3, f32[512]{0:T(512)S(1)} %add_rsqrt_fusion), kind=kOutput, calls=%fused_computation.97 | convolution fusion | flops 2155872256 | bytes 9455616 | tf_op jit(solution)/shard_map/dot_general | solution.py:101
  83.0 72.5 %all-gather.5.cloned.1.call-done = bf16[16384,257]{0,1:T(8,128)(2,1)} async-done(((bf16[512,257]{0,1:T(8,128)(2,1)}), bf16[16384,257]{0,1:T(8,128)(2,1)}) %all-gather.5.cloned.1.call-update) | async-done | bytes 8421392 | tf_op jit(solution)/shard_map/all_gather | solution.py:27
  155.5 5.8 %fusion.59 = (bf16[16384,128]{0,1:T(8,128)(2,1)}, bf16[16384,128]{0,1:T(8,128)(2,1)}) fusion(bf16[16384,257]{0,1:T(8,128)(2,1)} %all-gather.5.cloned.1.call-done), kind=kLoop, calls=%fused_computation.98 | loop fusion | bytes 16777216 | tf_op jit(solution)/shard_map/slice | solution.py:29
  162.5 173.0 %while.24 = (s32[]{:T(128)}, f32[1,4,256]{2,1,0:T(4,128)S(1)}, f32[1,4,256]{2,1,0:T(4,128)S(1)}, f32[1,4,256,128]{3,2,1,0:T(8,128)S(1)}, f32[1,4,256]{2,1,0:T(4,...) while((s32[]{:T(128)}, f32[1,4,256]{2,1,0:T(4,128)S(1)}, ...), condition=%wide.region_11.12_spmd.clone, body=%wide.region_2.11_spmd.clone.sunk | while | flops 549723392 | bytes 17977912 | solution.py:186
  176.7 2.0 conditional.6
  182.1 2.0 conditional.6
  187.5 2.0 conditional.6
  203.8 2.0 conditional.6
  209.2 2.0 conditional.6
  230.8 2.0 conditional.6
  236.2 2.0 conditional.6
  257.8 2.0 conditional.6
  263.2 2.0 conditional.6
  279.4 2.0 conditional.6
  284.9 2.0 conditional.6
  290.3 2.0 conditional.6
  306.5 2.0 conditional.6
  336.1 4.6 %convolution_convert_fusion = bf16[512,4096]{1,0:T(8,128)(2,1)S(1)} fusion(bf16[512,4096]{1,0:T(8,128)(2,1)} %param.18, bf16[256,512]{0,1:T(8,128)(2,1)S(1)} %bitcast.143, bf16[256,512]{0,1:T(8,128)(2,1)S(1)} %bitcast.142), kind=kOutput, calls=%fused_computation.57 | convolution fusion | flops 2150629376 | bytes 8912896 | tf_op jit(solution)/shard_map/dot_general | solution.py:197
  341.0 50.9 %all_to_all.11 = bf16[8,512,512]{2,1,0:T(8,128)(2,1)} all-to-all(bf16[8,512,512]{2,1,0:T(8,128)(2,1)S(1)} %bitcast.135), channel_id=1, replica_groups=mesh['cp'=32,'tp'=8] {'tp'}, dimensions={0} | all-to-all | bytes 8388608 | tf_op jit(solution)/shard_map/all_to_all | solution.py:43
  391.9 3.7 reduce_sum.54
  (767 shorter events, 285.4 us)
Async XLA Ops:
  6.5 57.5 %copy-start = (bf16[4096,128]{1,0:T(8,128)(2,1)S(1)}, bf16[4096,128]{1,0:T(8,128)(2,1)}, u32[]{:S(2)}) copy-start(bf16[4096,128]{1,0:T(8,128)(2,1)} %param.16) | copy-start | bytes 3145732
  6.5 57.5 %all-gather.3.cloned.1.call-start = ((), (), s32[]{:S(2)}) async-start(), calls=%async_computation.2 | async-start | bytes 4718592 | tf_op jit(solution)/shard_map/all_gather | solution.py:95
  9.1 9.7 %all-to-all-start = ((f32[8,1,512]{2,1,0:T(1,128)}), f32[8,1,512]{2,1,0:T(1,128)S(1)}, u32[]{:S(2)}, u32[]{:S(2)}) async-start(f32[8,1,512]{2,1,0:T(1,128)} %broadcast_in_dim.61), calls=%async_computation | async-start | bytes 32768 | tf_op jit(solution)/shard_map/all_to_all | solution.py:17
  13.7 141.7 %all-gather.5.cloned.1.call-start = ((), (), s32[]{:S(2)}) async-start(), calls=%async_computation.3 | async-start | bytes 8921088 | tf_op jit(solution)/shard_map/all_gather | solution.py:27
  18.8 49.7 %copy-start.2 = (bf16[4096,128]{1,0:T(8,128)(2,1)S(1)}, bf16[4096,128]{1,0:T(8,128)(2,1)}, u32[]{:S(2)}) copy-start(bf16[4096,128]{1,0:T(8,128)(2,1)} %param.17) | copy-start | bytes 3145732
  18.9 49.7 %copy-start.3 = (f32[4096]{0:T(1024)S(1)}, f32[4096]{0:T(1024)}, u32[]{:S(2)}) copy-start(f32[4096]{0:T(1024)} %param.14) | copy-start | bytes 49156
  64.0 4.5 %copy-start.1 = (bf16[512,4096]{1,0:T(8,128)(2,1)S(1)}, bf16[512,4096]{1,0:T(8,128)(2,1)}, u32[]{:S(2)}) copy-start(bf16[512,4096]{1,0:T(8,128)(2,1)} %all-gather.3.cloned.1.call-done) | copy-start | bytes 12582916
Sparse Core Ops, SparseCore 0:
  9.1 54.8 all-gather.2
  71.1 84.3 all-gather.4
where the time goes:
time: 403 us; the launch traced here: 402 us
  waiting for transfers between devices  123 us (31%)
  matrix products  97.4 us (24%)
  other arithmetic  58 us (14%)
  blocking collectives  50.9 us (13%)
  local copies, waits for them, and re-layouts  50.7 us (13%)
  between operations  13.6 us (3%)
  starting transfers between devices  4.68 us (1%)
  loops' own time  4.65 us (1%)
    all_gather x1, waiting for transfers between devices, in_one_piece(): out, at, done = (lax.all_gather(both, axis, axis=dim, tiled=True), 0, [])  72.5 us
    all_to_all x1, blocking collectives, sum_at_owner(): lax.all_to_all(tiles, axis, split_axis=0, concat_axis=0, tiled=True)  50.9 us
    dot_general x64, matrix products, attend_block(): jnp.einsum('sfec,csh->sfeh', attention_weights.astype(jnp.bfloat16), valu...  50.4 us
    all_gather x1, waiting for transfers between devices, shards(): piece = lax.all_gather(hidden, 'tp', axis=1, tiled=True)  45.1 us
    dynamic_slice x64, local copies, waits for them, and re-layouts, inner(): lax.dynamic_slice_in_dim(value_piece, offset, tok_rows, 0)  35.6 us
    dot_general x64, matrix products, attend_block(): jnp.einsum('ucpm,ycm->cpuy', query_matrix, key_matrix, preferred_element_...  30.9 us
    reduce_sum x64, other arithmetic, attend_block(): total = total * correction_scale + jnp.sum(attention_weights, axis=-1)  29.8 us
    and x64, other arithmetic, attend_block(): (key_pos[None, :] <= query_pos[:, None]) & (key_doc[None, :] == query_doc...  13.1 us
  transfers between devices with their start and end apart: 3, of which 3 were waited for; matrix products, arithmetic and copies ran while one was open for 4% of the time, Pallas kernels for 0%

commit v1 on v0

v1 whole, which is shorter than its diff:
```python
import math

import jax
import jax.numpy as jnp
import numpy as np
from jax import lax
from jax.experimental import pallas as pl
from jax.experimental.pallas import tpu as pltpu
from jax.sharding import PartitionSpec as P

HEADS = 32
KV_HEADS = 8
HEAD_SIZE = 128
LONGEST = 12288
DOCS = 6
TOK = 512
GROUP = 4
ROWS = GROUP * TOK
BLK = 2 * TOK + 16
PENALTY = -(2.0**100)
SCALE = math.log2(math.e) / math.sqrt(HEAD_SIZE)
QC = 256

epsilon = 1e-05
rope_base = 500000.0


WIDTH = 4096
PIECE = 512
N_TP = 8
CH = 4
CR = TOK // CH
MESH = pl.DeviceIdType.MESH


def tp_places():
    t = lax.axis_index("tp")
    plane = (t // 4) * 4
    y = t % 4
    up = plane + (y + 1) % 4
    down = plane + (y + 3) % 4
    far = plane + (y + 2) % 4
    return t, up, down, far


def other(t):
    return (t + 4) % 8


def greet(axis, peers):
    barrier = pltpu.get_barrier_semaphore()
    for peer in peers:
        pl.semaphore_signal(barrier, inc=1, device_id={axis: peer}, device_id_type=MESH)
    pl.semaphore_wait(barrier, len(peers))


def part(chunk):
    return pl.ds(chunk * CR, CR)


def project_kernel(
    h_ref, gain_ref, freq_ref, doc_ref, wq, wk, wv, q_out, kv_out,
    gath, w, acc, squares, cosine, sine, wsem, ssem, rsem, qssem, qrsem,
):
    t, up, down, far = tp_places()
    across = other(t)
    weights = [
        pltpu.make_async_copy(wq, w.at[:, 0:512], wsem.at[0]),
        pltpu.make_async_copy(wk, w.at[:, 512:640], wsem.at[1]),
        pltpu.make_async_copy(wv, w.at[:, 640:768], wsem.at[2]),
    ]
    for copy in weights:
        copy.start()
    peers = [(t + i) % N_TP for i in range(1, N_TP)]
    greet("tp", peers)
    sent = []

    def send(source, owner, chunk, to):
        copy = pltpu.make_async_remote_copy(
            src_ref=source,
            dst_ref=gath.at[owner, part(chunk)],
            send_sem=ssem.at[len(sent)],
            recv_sem=rsem.at[owner, chunk],
            device_id={"tp": to},
            device_id_type=MESH,
        )
        copy.start()
        sent.append(copy)

    def arrived(owner, chunk):
        pltpu.make_async_remote_copy(
            src_ref=gath.at[owner, part(chunk)],
            dst_ref=gath.at[owner, part(chunk)],
            send_sem=ssem.at[0],
            recv_sem=rsem.at[owner, chunk],
            device_id={"tp": across},
            device_id_type=MESH,
        ).wait_recv()

    upward = (0, 1, 2, 3)
    downward = (2, 3, 0, 1)

    def send_own(i):
        send(h_ref.at[part(upward[i])], t, upward[i], up)
        send(h_ref.at[part(downward[i])], t, downward[i], down)
        send(h_ref.at[part(upward[i])], t, upward[i], across)

    send_own(0)
    mine = h_ref[...].astype(jnp.float32)
    mass = jnp.sum(mine * mine, axis=1, keepdims=True)
    squares[t] = jnp.broadcast_to(mass, (TOK, 128)).T[0:8]
    told = []
    for i, peer in enumerate(peers):
        copy = pltpu.make_async_remote_copy(
            src_ref=squares.at[t],
            dst_ref=squares.at[t],
            send_sem=qssem.at[i],
            recv_sem=qrsem.at[t],
            device_id={"tp": peer},
            device_id_type=MESH,
        )
        copy.start()
        told.append(copy)
    for i in range(1, CH):
        send_own(i)

    first = lax.axis_index("cp") * TOK
    place = (first + lax.broadcasted_iota(jnp.int32, (HEAD_SIZE // 2, TOK), 1)).astype(jnp.float32)
    angle = place * freq_ref[...]
    cosine[...] = jnp.cos(angle)
    sine[...] = jnp.sin(angle)
    for peer in peers:
        pltpu.make_async_remote_copy(
            src_ref=squares.at[peer],
            dst_ref=squares.at[peer],
            send_sem=qssem.at[0],
            recv_sem=qrsem.at[peer],
            device_id={"tp": peer},
            device_id_type=MESH,
        ).wait_recv()
    whole = jnp.sum(squares[...], axis=0)[0:1]
    inverse = lax.rsqrt(whole / WIDTH + epsilon)
    inverse = jnp.broadcast_to(inverse, (128, TOK)).T
    inverse = jnp.concatenate([inverse] * (PIECE // 128), axis=1)
    for copy in weights:
        copy.wait()

    def use(source, owner, start):
        gain = gain_ref[pl.ds(owner, 1), :]
        normed = (source[...].astype(jnp.float32) * inverse * gain).astype(jnp.bfloat16)
        rows = pl.ds(pl.multiple_of(owner * PIECE, PIECE), PIECE)
        product = jnp.dot(normed, w[rows, :], preferred_element_type=jnp.float32)
        if start:
            acc[...] = product
        else:
            acc[...] += product

    use(h_ref, t, True)
    for i in range(CH):
        arrived(down, upward[i])
        if i < 2:
            send(gath.at[down, part(upward[i])], down, upward[i], up)
        arrived(up, downward[i])
        if i < 2:
            send(gath.at[up, part(downward[i])], up, downward[i], down)
        arrived(across, upward[i])
        if i == 1:
            for chunk in (0, 1):
                send(gath.at[across, part(chunk)], across, chunk, up)
                send(gath.at[across, part(chunk)], across, chunk, down)
        if i > 1:
            send(gath.at[across, part(i)], across, i, up)
            send(gath.at[across, part(i)], across, i, down)
    use(gath.at[up], up, False)
    use(gath.at[down], down, False)
    for i in range(2):
        for chunk in (upward[i], downward[i]):
            arrived(far, chunk)
            send(gath.at[far, part(chunk)], far, chunk, across)
    use(gath.at[across], across, False)
    use(gath.at[far], far, False)
    for chunk in (0, 2, 1, 3):
        arrived(other(far), chunk)
    use(gath.at[other(far)], other(far), False)
    for side in (up, down):
        for chunk in range(CH):
            arrived(other(side), chunk)
        use(gath.at[other(side)], other(side), False)

    half = HEAD_SIZE // 2
    for head in range(GROUP + 1):
        raw = acc[:, head * HEAD_SIZE : (head + 1) * HEAD_SIZE].T
        a = raw[:half]
        b = raw[half:]
        low = a * cosine[...] - b * sine[...]
        high = b * cosine[...] + a * sine[...]
        if head < GROUP:
            cols = slice(head * TOK, (head + 1) * TOK)
            q_out[0:half, cols] = low.astype(jnp.bfloat16)
            q_out[half:, cols] = high.astype(jnp.bfloat16)
        else:
            turned = jnp.concatenate([low, high], axis=0).T
            kv_out[0:TOK, :] = turned.astype(jnp.bfloat16)
    value = acc[:, (GROUP + 1) * HEAD_SIZE :].T.astype(jnp.bfloat16)
    for i in range(TOK // 128):
        kv_out[TOK + 128 * i : TOK + 128 * (i + 1), :] = value[:, 128 * i : 128 * (i + 1)]
    lane = lax.broadcasted_iota(jnp.int32, (16, 128), 1)
    row = lax.broadcasted_iota(jnp.int32, (16, 128), 0)
    tail = jnp.zeros((16, 128), jnp.int32)
    for d in range(1, DOCS):
        count = jnp.sum(jnp.where(doc_ref[...] < d, 1, 0), axis=1, keepdims=True)
        tail = jnp.where(
            (lane == d) & (row == 0), count // 16, jnp.where((lane == d) & (row == 1), count % 16, tail)
        )
    kv_out[2 * TOK :, :] = tail.astype(jnp.float32).astype(jnp.bfloat16)
    for copy in sent + told:
        copy.wait_send()


def project(hidden, norm_gain, w_query, w_key, w_value, doc_ids):
    vmem = pl.BlockSpec(memory_space=pltpu.VMEM)
    hbm = pl.BlockSpec(memory_space=pl.ANY)
    powers = -np.arange(HEAD_SIZE // 2, dtype=np.float32) * np.float32(2.0) / HEAD_SIZE
    freqs = (np.float64(rope_base) ** powers.astype(np.float64)).astype(np.float32)
    freqs = jnp.asarray(np.broadcast_to(freqs[:, None], (HEAD_SIZE // 2, TOK)))
    return pl.pallas_call(
        project_kernel,
        out_shape=(
            jax.ShapeDtypeStruct((HEAD_SIZE, ROWS), jnp.bfloat16),
            jax.ShapeDtypeStruct((BLK, 128), jnp.bfloat16),
        ),
        in_specs=[vmem] * 4 + [hbm] * 3,
        out_specs=(vmem, vmem),
        scratch_shapes=[
            pltpu.VMEM((N_TP, TOK, PIECE), jnp.bfloat16),
            pltpu.VMEM((WIDTH, 768), jnp.bfloat16),
            pltpu.VMEM((TOK, 768), jnp.float32),
            pltpu.VMEM((N_TP, 8, TOK), jnp.float32),
            pltpu.VMEM((HEAD_SIZE // 2, TOK), jnp.float32),
            pltpu.VMEM((HEAD_SIZE // 2, TOK), jnp.float32),
            pltpu.SemaphoreType.DMA((3,)),
            pltpu.SemaphoreType.DMA((28,)),
            pltpu.SemaphoreType.DMA((N_TP, CH)),
            pltpu.SemaphoreType.DMA((N_TP - 1,)),
            pltpu.SemaphoreType.DMA((N_TP,)),
        ],
        compiler_params=pltpu.CompilerParams(
            collective_id=0, has_side_effects=True, vmem_limit_bytes=48 * 2**20
        ),
        name="project",
    )(hidden, norm_gain.reshape(N_TP, PIECE), freqs, doc_ids, w_query, w_key, w_value)


def combine_kernel(
    att, w_out, out_ref,
    w, terms, sums, across_in, side_in, half_in, side_end, across_end,
    wsem, ssem, rsem,
):
    t, up, down, far = tp_places()
    across = other(t)
    order = [other(far), other(up), other(down), far, across, up, down, t]
    weights = []
    for i, owner in enumerate(order):
        cols = pl.ds(pl.multiple_of(owner * PIECE, PIECE), PIECE)
        weights.append(pltpu.make_async_copy(w_out.at[:, cols], w.at[i], wsem.at[i]))
        weights[-1].start()
    greet("tp", (up, down, across))
    sent = []

    def send(source, target, number, to):
        copy = pltpu.make_async_remote_copy(
            src_ref=source,
            dst_ref=target,
            send_sem=ssem.at[len(sent)],
            recv_sem=rsem.at[number],
            device_id={"tp": to},
            device_id_type=MESH,
        )
        copy.start()
        sent.append(copy)

    def arrived(target, number):
        pltpu.make_async_remote_copy(
            src_ref=target,
            dst_ref=target,
            send_sem=ssem.at[0],
            recv_sem=rsem.at[number],
            device_id={"tp": across},
            device_id_type=MESH,
        ).wait_recv()
        return target[...].astype(jnp.float32)

    def compute(i):
        weights[i].wait()
        product = jnp.dot(att[...], w[i], preferred_element_type=jnp.float32)
        terms[i] = product.astype(jnp.bfloat16)

    def term(i, chunk):
        return terms[i, part(chunk)].astype(jnp.float32)

    UP, DOWN = 0, 1
    compute(0)
    for chunk in (0, 2, 1, 3):
        send(terms.at[0, part(chunk)], across_in.at[part(chunk)], chunk, across)
    compute(1)
    compute(2)
    for chunk in range(CH):
        send(terms.at[1, part(chunk)], side_in.at[DOWN, part(chunk)], 4 + chunk, up)
        send(terms.at[2, part(chunk)], side_in.at[UP, part(chunk)], 8 + chunk, down)
    for i in range(3, 8):
        compute(i)
    for chunk in (0, 2, 1, 3):
        got = arrived(across_in.at[part(chunk)], chunk)
        sums[0, part(chunk)] = (term(3, chunk) + got).astype(jnp.bfloat16)
        if chunk < 2:
            send(sums.at[0, part(chunk)], half_in.at[DOWN, part(chunk)], 12 + chunk, up)
        else:
            send(sums.at[0, part(chunk)], half_in.at[UP, part(chunk - 2)], 12 + chunk, down)
    for chunk in range(CH):
        below = arrived(side_in.at[DOWN, part(chunk)], 4 + chunk)
        above = arrived(side_in.at[UP, part(chunk)], 8 + chunk)
        sums[1, part(chunk)] = (term(4, chunk) + below + above).astype(jnp.bfloat16)
        send(sums.at[1, part(chunk)], across_end.at[part(chunk)], 16 + chunk, across)
    for i in range(2):
        send(terms.at[5, part(2 + i)], side_end.at[DOWN, part(2 + i)], 22 + i, up)
        send(terms.at[6, part(i)], side_end.at[UP, part(i)], 24 + i, down)
    for i in range(2):
        got = arrived(half_in.at[DOWN, part(i)], 12 + i)
        sums[2, part(i)] = (term(5, i) + got).astype(jnp.bfloat16)
        send(sums.at[2, part(i)], side_end.at[DOWN, part(i)], 20 + i, up)
        got = arrived(half_in.at[UP, part(i)], 14 + i)
        sums[3, part(2 + i)] = (term(6, 2 + i) + got).astype(jnp.bfloat16)
        send(sums.at[3, part(2 + i)], side_end.at[UP, part(2 + i)], 26 + i, down)
    for chunk in range(CH):
        total = term(7, chunk) + arrived(across_end.at[part(chunk)], 16 + chunk)
        total = total + arrived(side_end.at[DOWN, part(chunk)], 20 + chunk)
        total = total + arrived(side_end.at[UP, part(chunk)], 24 + chunk)
        out_ref[part(chunk), :] = total.astype(jnp.bfloat16)
    for copy in sent:
        copy.wait_send()


def combine(attended, w_out):
    vmem = pl.BlockSpec(memory_space=pltpu.VMEM)
    hbm = pl.BlockSpec(memory_space=pl.ANY)
    return pl.pallas_call(
        combine_kernel,
        out_shape=jax.ShapeDtypeStruct((TOK, PIECE), jnp.bfloat16),
        in_specs=[vmem, hbm],
        out_specs=vmem,
        scratch_shapes=[
            pltpu.VMEM((N_TP, PIECE, PIECE), jnp.bfloat16),
            pltpu.VMEM((N_TP, TOK, PIECE), jnp.bfloat16),
            pltpu.VMEM((4, TOK, PIECE), jnp.bfloat16),
            pltpu.VMEM((TOK, PIECE), jnp.bfloat16),
            pltpu.VMEM((2, TOK, PIECE), jnp.bfloat16),
            pltpu.VMEM((2, TOK // 2, PIECE), jnp.bfloat16),
            pltpu.VMEM((2, TOK, PIECE), jnp.bfloat16),
            pltpu.VMEM((TOK, PIECE), jnp.bfloat16),
            pltpu.SemaphoreType.DMA((N_TP,)),
            pltpu.SemaphoreType.DMA((28,)),
            pltpu.SemaphoreType.DMA((28,)),
        ],
        compiler_params=pltpu.CompilerParams(
            collective_id=1, has_side_effects=True, vmem_limit_bytes=40 * 2**20
        ),
        name="combine",
    )(attended, w_out)


def augment_queries(q_ref, doc_ref, qaug):
    qaug[0:HEAD_SIZE, :] = q_ref[...]
    row = lax.broadcasted_iota(jnp.int32, (HEAD_SIZE, TOK), 0)
    hot = jnp.where(row == doc_ref[...], PENALTY, 0.0).astype(jnp.bfloat16)
    for head in range(GROUP):
        qaug[HEAD_SIZE:, head * TOK : (head + 1) * TOK] = hot


def attend(block, qaug, best, total, acc, first):
    keys = block[0:TOK, :]
    counts = block[2 * TOK : 2 * TOK + 2, :].astype(jnp.float32)
    below = counts[0:1] * 16.0 + counts[1:2]
    row = lax.broadcasted_iota(jnp.int32, (TOK, HEAD_SIZE), 0).astype(jnp.float32)
    earlier = jnp.where(row < below, 1.0, 0.0).astype(jnp.bfloat16)
    keys = jnp.concatenate([keys, earlier], axis=1)
    values = jnp.concatenate(
        [block[TOK + 128 * i : TOK + 128 * (i + 1), :] for i in range(TOK // 128)], axis=1
    )
    for chunk in range(ROWS // QC):
        cols = slice(chunk * QC, (chunk + 1) * QC)
        scores = jnp.dot(keys, qaug[:, cols], preferred_element_type=jnp.float32)
        if first:
            key_at = lax.broadcasted_iota(jnp.int32, (TOK, QC), 0)
            query_at = lax.broadcasted_iota(jnp.int32, (TOK, QC), 1) + (chunk * QC) % TOK
            scores = jnp.where(key_at <= query_at, scores, jnp.float32(PENALTY))
            top = jnp.max(scores, axis=0, keepdims=True)
        else:
            old = best[:, cols]
            top = jnp.maximum(old, jnp.max(scores, axis=0, keepdims=True))
        weights = jnp.exp2(scores * SCALE - top * SCALE)
        mass = jnp.sum(weights, axis=0, keepdims=True)
        out = jnp.dot(values, weights.astype(jnp.bfloat16), preferred_element_type=jnp.float32)
        if first:
            total[:, cols] = mass
            acc[:, cols] = out
        else:
            shrink = jnp.exp2((old - top) * SCALE)
            total[:, cols] = total[:, cols] * shrink + mass
            acc[:, cols] = acc[:, cols] * shrink + out
        best[:, cols] = top


def finish(total, acc, out_ref):
    for head in range(GROUP):
        cols = slice(head * TOK, (head + 1) * TOK)
        out_ref[:, head * HEAD_SIZE : (head + 1) * HEAD_SIZE] = (
            (acc[:, cols] / total[:, cols]).T.astype(jnp.bfloat16)
        )


def attention_kernel(q_ref, doc_ref, kv_ref, out_ref, qaug, best, total, acc):
    me = lax.axis_index("cp")
    augment_queries(q_ref, doc_ref, qaug)
    attend(kv_ref.at[me], qaug, best, total, acc, True)

    @pl.loop(jnp.maximum(me - LONGEST // TOK, 0), me)
    def _(j):
        attend(kv_ref.at[j], qaug, best, total, acc, False)

    finish(total, acc, out_ref)


def attention(queries, docs, blocks):
    vmem = pl.BlockSpec(memory_space=pltpu.VMEM)
    return pl.pallas_call(
        attention_kernel,
        out_shape=jax.ShapeDtypeStruct((TOK, GROUP * HEAD_SIZE), jnp.bfloat16),
        in_specs=[vmem] * 3,
        out_specs=vmem,
        scratch_shapes=[
            pltpu.VMEM((2 * HEAD_SIZE, ROWS), jnp.bfloat16),
            pltpu.VMEM((1, ROWS), jnp.float32),
            pltpu.VMEM((1, ROWS), jnp.float32),
            pltpu.VMEM((HEAD_SIZE, ROWS), jnp.float32),
        ],
        compiler_params=pltpu.CompilerParams(vmem_limit_bytes=40 * 2**20),
        name="attention",
    )(queries, docs, blocks)


def shards(hidden, norm_gain, w_query, w_key, w_value, w_out, doc_ids):
    docs = doc_ids.reshape(1, TOK)
    queries, block = project(hidden, norm_gain, w_query, w_key, w_value, docs)
    blocks = lax.all_gather(block, "cp", axis=0, tiled=False)
    attended = attention(queries, docs, blocks)
    return combine(attended, w_out)


def solution(mesh):
    in_specs = (
        P("cp", "tp"),
        P(),
        P(None, "tp"),
        P(None, "tp"),
        P(None, "tp"),
        P("tp", None),
        P("cp"),
    )
    return jax.shard_map(
        shards, mesh=mesh, in_specs=in_specs, out_specs=P("cp", "tp"), check_vma=False
    )
```

time: 403 us -> 264 us (0.66)
  the two profiles are of different devices: /device:TPU:199 before, /device:TPU:224 now
where the time goes in v1:
time: 264 us; the launch traced here: 263 us
  Pallas kernels  163 us (62%)
  waiting for transfers between devices  77.1 us (29%)
  between operations  13.4 us (5%)
  local copies, waits for them, and re-layouts  9.85 us (4%)
    pallas_call x1, Pallas kernels, attention(): pl.pallas_call(attention_kernel, out_shape=jax.ShapeDtypeStruct((TOK, GRO...  89 us
    all_gather x1, waiting for transfers between devices, shards(): blocks = lax.all_gather(block, 'cp', axis=0, tiled=False)  77 us
    pallas_call x1, Pallas kernels, project(): pl.pallas_call(project_kernel, out_shape=(jax.ShapeDtypeStruct((HEAD_SIZE...  37.6 us
    pallas_call x1, Pallas kernels, combine(): pl.pallas_call(combine_kernel, out_shape=jax.ShapeDtypeStruct((TOK, PIECE...  36.3 us
    unnamed x15, local copies, waits for them, and re-layouts  8.39 us
  transfers between devices with their start and end apart: 1, of which 1 were waited for; matrix products, arithmetic and copies ran while one was open for 0% of the time, Pallas kernels for 0%

profile of v1, /device:TPU:224, one launch (start us, length us, event | category | flops | bytes accessed | tf_op | source)
XLA Modules:
  0.0 263.2 jit_solution(2482076285551143854)
XLA Ops:
  6.5 0.0 copy-start.6
  6.5 0.0 all-gather.3.cloned.1.call-start
  6.5 0.7 reshape.6.gain_ref
  7.3 0.7 jit_solution_.3.freq_ref
  8.0 0.0 copy-start.2
  8.0 1.2 copy-done.2
  9.2 0.0 copy-start.3
  9.2 1.2 copy-done.3
  10.5 0.0 copy-start.4
  10.5 1.0 copy-done.4
  11.5 0.0 copy-start.5
  11.5 0.7 copy-done.5
  12.2 37.6 %project.1 = (bf16[128,2048]{1,0:T(8,128)(2,1)S(1)}, bf16[1040,128]{1,0:T(8,128)(2,1)}) custom-call(bf16[512,512]{1,0:T(8,128)(2,1)S(1)} %copy-done.4, f32[8,512]{1,0:T(8,128)S(1)} %reshape.6.gain_ref, f32[64,512]{1,0:T(8,128)S(1)} %jit_solution_.3.freq_ref, s32[1,512]{1,0:T(1,128)S(1)} %bitcast.3, bf16[4096,512]{1,0:T(8,128)(2,1)} %wq.1, ...), custom_call_target="tpu_custom_call" | custom-call | tf_op jit(solution)/shard_map/project/pallas_call | solution.py:226
  49.8 0.0 all-gather.3.cloned.1.call-update
  49.8 77.0 %all-gather.3.cloned.1.call-done = bf16[33280,128]{1,0:T(8,128)(2,1)} async-done(((bf16[1040,128]{1,0:T(8,128)(2,1)}), bf16[33280,128]{1,0:T(8,128)(2,1)}) %all-gather.3.cloned.1.call-update) | async-done | bytes 8519696 | tf_op jit(solution)/shard_map/all_gather | solution.py:454
  126.8 0.0 copy-done.6
  126.8 0.0 copy-start
  126.8 3.4 %copy-done = bf16[33280,128]{1,0:T(8,128)(2,1)S(1)} copy-done((bf16[33280,128]{1,0:T(8,128)(2,1)S(1)}, bf16[33280,128]{1,0:T(8,128)(2,1)}, u32[]{:S(2)}) %copy-start) | copy-done | bytes 8519704
  130.2 0.0 copy-start.1
  130.3 89.0 %attention.1.att = bf16[512,512]{1,0:T(8,128)(2,1)S(1)} custom-call(bf16[128,2048]{1,0:T(8,128)(2,1)S(1)} %get-tuple-element.7.q_ref, s32[1,512]{1,0:T(1,128)S(1)} %bitcast.4, bf16[32,1040,128]{2,1,0:T(8,128)(2,1)S(1)} %bitcast.2), custom_call_target="tpu_custom_call" | custom-call | tf_op jit(solution)/shard_map/attention/pallas_call | solution.py:435
  219.2 0.0 copy-done.1
  219.3 36.3 %combine.1 = bf16[512,512]{1,0:T(8,128)(2,1)S(1)} custom-call(bf16[512,512]{1,0:T(8,128)(2,1)S(1)} %attention.1.att, bf16[512,4096]{1,0:T(8,128)(2,1)S(1)} %copy-done.1), custom_call_target="tpu_custom_call" | custom-call | tf_op jit(solution)/shard_map/combine/pallas_call | solution.py:346
  255.6 0.8 copy.10
Async XLA Ops:
  6.5 120.3 %copy-start.6 = (s32[512]{0:T(512)S(1)}, s32[512]{0:T(512)}, u32[]{:S(2)}) copy-start(s32[512]{0:T(512)} %param.14) | copy-start | bytes 6148
  6.5 120.3 %all-gather.3.cloned.1.call-start = ((), (), s32[]{:S(2)}) async-start(), calls=%async_computation | async-start | bytes 8785920 | tf_op jit(solution)/shard_map/all_gather | solution.py:454
  8.0 1.2 copy-start.2
  9.2 1.2 copy-start.3
  10.5 1.0 copy-start.4
  11.5 0.7 copy-start.5
  126.8 3.4 %copy-start = (bf16[33280,128]{1,0:T(8,128)(2,1)S(1)}, bf16[33280,128]{1,0:T(8,128)(2,1)}, u32[]{:S(2)}) copy-start(bf16[33280,128]{1,0:T(8,128)(2,1)} %all-gather.3.cloned.1.call-done) | copy-start | bytes 25559044
  130.2 89.0 %copy-start.1 = (bf16[512,4096]{1,0:T(8,128)(2,1)S(1)}, bf16[512,4096]{1,0:T(8,128)(2,1)}, u32[]{:S(2)}) copy-start(bf16[512,4096]{1,0:T(8,128)(2,1)} %w_out.1) | copy-start | bytes 12582916
Sparse Core Ops, SparseCore 0:
  49.9 76.8 all-gather.2

commit v2 on v1

--- a/solution.py
+++ b/solution.py
@@ -19,7 +19,7 @@
 BLK = 2 * TOK + 16
 PENALTY = -(2.0**100)
 SCALE = math.log2(math.e) / math.sqrt(HEAD_SIZE)
-QC = 256
+QC = 512
 
 epsilon = 1e-05
 rope_base = 500000.0
@@ -376,38 +376,61 @@
         qaug[HEAD_SIZE:, head * TOK : (head + 1) * TOK] = hot
 
 
-def attend(block, qaug, best, total, acc, first):
-    keys = block[0:TOK, :]
+def attend_keys(block):
     counts = block[2 * TOK : 2 * TOK + 2, :].astype(jnp.float32)
     below = counts[0:1] * 16.0 + counts[1:2]
     row = lax.broadcasted_iota(jnp.int32, (TOK, HEAD_SIZE), 0).astype(jnp.float32)
     earlier = jnp.where(row < below, 1.0, 0.0).astype(jnp.bfloat16)
-    keys = jnp.concatenate([keys, earlier], axis=1)
-    values = jnp.concatenate(
-        [block[TOK + 128 * i : TOK + 128 * (i + 1), :] for i in range(TOK // 128)], axis=1
-    )
-    for chunk in range(ROWS // QC):
-        cols = slice(chunk * QC, (chunk + 1) * QC)
-        scores = jnp.dot(keys, qaug[:, cols], preferred_element_type=jnp.float32)
-        if first:
-            key_at = lax.broadcasted_iota(jnp.int32, (TOK, QC), 0)
-            query_at = lax.broadcasted_iota(jnp.int32, (TOK, QC), 1) + (chunk * QC) % TOK
-            scores = jnp.where(key_at <= query_at, scores, jnp.float32(PENALTY))
-            top = jnp.max(scores, axis=0, keepdims=True)
-        else:
-            old = best[:, cols]
-            top = jnp.maximum(old, jnp.max(scores, axis=0, keepdims=True))
-        weights = jnp.exp2(scores * SCALE - top * SCALE)
-        mass = jnp.sum(weights, axis=0, keepdims=True)
-        out = jnp.dot(values, weights.astype(jnp.bfloat16), preferred_element_type=jnp.float32)
-        if first:
-            total[:, cols] = mass
-            acc[:, cols] = out
-        else:
-            shrink = jnp.exp2((old - top) * SCALE)
-            total[:, cols] = total[:, cols] * shrink + mass
-            acc[:, cols] = acc[:, cols] * shrink + out
-        best[:, cols] = top
+    return jnp.concatenate([block[0:TOK, :], earlier], axis=1)
+
+
+def score(keys, chunk, qaug, logits, tops, causal):
+    cols = slice(chunk * QC, (chunk + 1) * QC)
+    scores = jnp.dot(keys, qaug[:, cols], preferred_element_type=jnp.float32)
+    if causal:
+        key_at = lax.broadcasted_iota(jnp.int32, (TOK, QC), 0)
+        query_at = lax.broadcasted_iota(jnp.int32, (TOK, QC), 1) + (chunk * QC) % TOK
+        scores = jnp.where(key_at <= query_at, scores, jnp.float32(PENALTY))
+    logits[chunk % 2] = scores
+    tops[chunk % 2] = jnp.max(scores, axis=0, keepdims=True)
+
+
+def weigh(values, chunk, logits, tops, best, total, acc, first):
+    cols = slice(chunk * QC, (chunk + 1) * QC)
+    top = tops[chunk % 2]
+    if not first:
+        old = best[:, cols]
+        top = jnp.maximum(old, top)
+    weights = jnp.exp2(logits[chunk % 2] * SCALE - top * SCALE)
+    mass = jnp.sum(weights, axis=0, keepdims=True)
+    out = jnp.dot(values, weights.astype(jnp.bfloat16), preferred_element_type=jnp.float32)
+    if first:
+        total[:, cols] = mass
+        acc[:, cols] = out
+    else:
+        shrink = jnp.exp2((old - top) * SCALE)
+        total[:, cols] = total[:, cols] * shrink + mass
+        acc[:, cols] = acc[:, cols] * shrink + out
+    best[:, cols] = top
+
+
+def attend(blocks, state, first):
+    qaug, logits, tops, best, total, acc = state
+    chunks = ROWS // QC
+    keys = [attend_keys(block) for block in blocks]
+    values = [
+        jnp.concatenate(
+            [block[TOK + 128 * i : TOK + 128 * (i + 1), :] for i in range(TOK // 128)], axis=1
+        )
+        for block in blocks
+    ]
+    score(keys[0], 0, qaug, logits, tops, first)
+    for step in range(len(blocks) * chunks):
+        if step + 1 < len(blocks) * chunks:
+            which, chunk = divmod(step + 1, chunks)
+            score(keys[which], chunk, qaug, logits, tops, first)
+        which, chunk = divmod(step, chunks)
+        weigh(values[which], chunk, logits, tops, best, total, acc, first)
 
 
 def finish(total, acc, out_ref):
@@ -418,19 +441,172 @@
         )
 
 
-def attention_kernel(q_ref, doc_ref, kv_ref, out_ref, qaug, best, total, acc):
+ROLES = 15
+PARTS = ((0, TOK), (TOK, TOK + 16))
+
+
+def attention_kernel(
+    q_ref, doc_ref, own_ref, out_ref,
+    kv, qaug, logits, tops, best, total, acc, ssem, rsem, sibsend, sibrecv,
+):
     me = lax.axis_index("cp")
+    core = me % 2
+    x = (me // 2) % 4
+    z = me // 8
+    state = (qaug, logits, tops, best, total, acc)
+
+    def at(zz, xx):
+        return (zz * 4 + xx) * 2 + core
+
+    right = at(z, (x + 1) % 4)
+    left = at(z, (x + 3) % 4)
+    ahead = at((z + 1) % 4, x)
+    behind = at((z + 3) % 4, x)
+    sibling = me + 1 - 2 * core
+    greet("cp", (right, left, ahead, behind, sibling))
+
+    def move(source, slot, half, to, send_sem, recv_sem):
+        rows = pl.ds(*PARTS[half])
+        return pltpu.make_async_remote_copy(
+            src_ref=source.at[rows],
+            dst_ref=kv.at[slot, rows],
+            send_sem=send_sem,
+            recv_sem=recv_sem,
+            device_id={"cp": to},
+            device_id_type=MESH,
+        )
+
+    always = z >= 0
+    top = z == 3
+    one, two = z >= 1, z >= 2
+    xm, xp, x2 = (x + 3) % 4, (x + 1) % 4, (x + 2) % 4
+    roles = [
+        (x >= 1, z, xm),
+        (x == 3, z, xp),
+        (x >= 2, z, x2),
+        (one, (z + 3) % 4, x),
+        (top, 0 * z, x),
+        (one, (z + 3) % 4, xm),
+        (one, (z + 3) % 4, xp),
+        (top & (x < 3), 0 * z, xp),
+        (top & (x == 0), 0 * z, xm),
+        (one, (z + 3) % 4, x2),
+        (top & (x < 2), 0 * z, x2),
+        (two, (z + 2) % 4, x),
+        (two, (z + 2) % 4, xm),
+        (two, (z + 2) % 4, xp),
+        (two, (z + 2) % 4, x2),
+    ]
+    slots = [at(zz, xx) for _, zz, xx in roles]
+    middle = (x == 1) | (x == 2)
+    forwards = {
+        0: [(middle, right, (0, 1))],
+        3: [(z < 3, ahead, (0, 1)), (always, right, (0, 1)), (always, left, (1, 0))],
+        4: [(x > 0, left, (0, 1)), (x == 3, right, (0, 1))],
+        5: [(always, right, (0,))],
+        6: [(always, left, (1,))],
+        7: [(middle, left, (0, 1))],
+        11: [(always, right, (0, 1)), (always, left, (1, 0))],
+        12: [(always, right, (0,))],
+        13: [(always, left, (1,))],
+    }
+    sends = []
+
+    def plan(when, source, slot, half, to):
+        number = len(sends)
+        sends.append((when, source, slot, half, to))
+        return number
+
+    def issue(number):
+        when, source, slot, half, to = sends[number]
+
+        @pl.when(when)
+        def _():
+            move(source, slot, half, to, ssem.at[number], rsem.at[slot, half]).start()
+
+    own = []
+    for half in (0, 1):
+        own.append(plan(z < 3, own_ref, me, half, ahead))
+        own.append(plan(z == 0, own_ref, me, half, behind))
+        own.append(plan(x < 3, own_ref, me, half, right))
+        own.append(plan(x == 0, own_ref, me, half, left))
+    relays = {}
+    for role, targets in forwards.items():
+        relays[role] = {0: [], 1: []}
+        for when, to, halves in targets:
+            for half in halves:
+                number = plan(roles[role][0] & when, kv.at[slots[role]], slots[role], half, to)
+                relays[role][half].append(number)
+
+    for half in (0, 1):
+        move(own_ref, me, half, sibling, sibsend.at[ROLES, half], sibrecv.at[ROLES, half]).start()
+    for number in own:
+        issue(number)
     augment_queries(q_ref, doc_ref, qaug)
-    attend(kv_ref.at[me], qaug, best, total, acc, True)
-
-    @pl.loop(jnp.maximum(me - LONGEST // TOK, 0), me)
-    def _(j):
-        attend(kv_ref.at[j], qaug, best, total, acc, False)
+    attend([own_ref], state, True)
+    for half in (0, 1):
+        move(own_ref, sibling, half, sibling, sibsend.at[ROLES, half], sibrecv.at[ROLES, half]).wait_recv()
+
+    @pl.when(core == 1)
+    def _():
+        attend([kv.at[sibling]], state, False)
+
+    def serve(role):
+        slot = slots[role]
+        for half in (0, 1):
+
+            @pl.when(roles[role][0])
+            def _():
+                move(own_ref, slot, half, sibling, ssem.at[0], rsem.at[slot, half]).wait_recv()
+                move(
+                    kv.at[slot], slot, half, sibling, sibsend.at[role, half], sibrecv.at[role, half]
+                ).start()
+
+            for number in relays.get(role, {0: [], 1: []})[half]:
+                issue(number)
+
+    @pl.loop(0, ROLES)
+    def _(step):
+        there = step < 0
+        slot = 0 * step
+        for role in range(ROLES):
+
+            @pl.when(step == role)
+            def _():
+                serve(role)
+
+            there = there | ((step == role) & roles[role][0])
+            slot = jnp.where(step == role, slots[role], slot)
+
+        @pl.when(there)
+        def _():
+            twin = slot + 1 - 2 * core
+            for half in (0, 1):
+                move(own_ref, twin, half, sibling, sibsend.at[step, half], sibrecv.at[step, half]).wait_recv()
+            attend([kv.at[slot], kv.at[twin]], state, False)
 
     finish(total, acc, out_ref)
-
-
-def attention(queries, docs, blocks):
+    for number, (when, source, slot, half, to) in enumerate(sends):
+
+        @pl.when(when)
+        def _():
+            move(source, slot, half, to, ssem.at[number], rsem.at[slot, half]).wait_send()
+
+    for role in range(ROLES + 1):
+        present, slot = (always, me) if role == ROLES else (roles[role][0], slots[role])
+        for half in (0, 1):
+
+            @pl.when(present)
+            def _():
+                move(
+                    own_ref, slot, half, sibling, sibsend.at[role, half], sibrecv.at[role, half]
+                ).wait_send()
+
+
+SENDS = 30
+
+
+def attention(queries, docs, block):
     vmem = pl.BlockSpec(memory_space=pltpu.VMEM)
     return pl.pallas_call(
         attention_kernel,
@@ -438,21 +614,29 @@
         in_specs=[vmem] * 3,
         out_specs=vmem,
         scratch_shapes=[
+            pltpu.VMEM((32, BLK, 128), jnp.bfloat16),
             pltpu.VMEM((2 * HEAD_SIZE, ROWS), jnp.bfloat16),
+            pltpu.VMEM((2, TOK, QC), jnp.float32),
+            pltpu.VMEM((2, 1, QC), jnp.float32),
             pltpu.VMEM((1, ROWS), jnp.float32),
             pltpu.VMEM((1, ROWS), jnp.float32),
             pltpu.VMEM((HEAD_SIZE, ROWS), jnp.float32),
+            pltpu.SemaphoreType.DMA((SENDS,)),
+            pltpu.SemaphoreType.DMA((32, 2)),
+            pltpu.SemaphoreType.DMA((ROLES + 1, 2)),
+            pltpu.SemaphoreType.DMA((ROLES + 1, 2)),
         ],
-        compiler_params=pltpu.CompilerParams(vmem_limit_bytes=40 * 2**20),
+        compiler_params=pltpu.CompilerParams(
+            collective_id=2, has_side_effects=True, vmem_limit_bytes=40 * 2**20
+        ),
         name="attention",
-    )(queries, docs, blocks)
+    )(queries, docs, block)
 
 
 def shards(hidden, norm_gain, w_query, w_key, w_value, w_out, doc_ids):
     docs = doc_ids.reshape(1, TOK)
     queries, block = project(hidden, norm_gain, w_query, w_key, w_value, docs)
-    blocks = lax.all_gather(block, "cp", axis=0, tiled=False)
-    attended = attention(queries, docs, blocks)
+    attended = attention(queries, docs, block)
     return combine(attended, w_out)
 
 

time: 264 us -> 158 us (0.60)
  waiting for transfers between devices: 77.1 us -> 0 us
  between operations: 13.4 us -> 0.05 us
  Pallas kernels: 163 us -> 150 us
  local copies, waits for them, and re-layouts: 9.85 us -> 6.77 us
    all_gather x1 -> x0, waiting for transfers between devices: 77 us -> none  [shards(): blocks = lax.all_gather(block, 'cp', axis=0, tiled=False)]
    pallas_call x1, Pallas kernels: 89 us -> 77.5 us  [attention(): pl.pallas_call(attention_kernel, out_shape=jax.ShapeDtypeStruct((TOK, GRO...]
    unnamed x15 -> x11, local copies, waits for them, and re-layouts: 8.39 us -> 5.17 us
  transfers between devices with their start and end apart: 1 -> 0, of which waited for: 1 -> 0; matrix products, arithmetic and copies ran while one was open for 0% -> 0% of each run, Pallas kernels for 0% -> 0%
where the time goes in v2:
time: 158 us; the launch traced here: 157 us
  Pallas kernels  150 us (95%)
  local copies, waits for them, and re-layouts  6.77 us (4%)
    pallas_call x1, Pallas kernels, attention(): pl.pallas_call(attention_kernel, out_shape=jax.ShapeDtypeStruct((TOK, GRO...  77.5 us
    pallas_call x1, Pallas kernels, project(): pl.pallas_call(project_kernel, out_shape=(jax.ShapeDtypeStruct((HEAD_SIZE...  37 us
    pallas_call x1, Pallas kernels, combine(): pl.pallas_call(combine_kernel, out_shape=jax.ShapeDtypeStruct((TOK, PIECE...  35.6 us
    unnamed x11, local copies, waits for them, and re-layouts  5.17 us

profile of v2, /device:TPU:224, one launch (start us, length us, event | category | flops | bytes accessed | tf_op | source)
XLA Modules:
  0.0 156.9 jit_solution(13042207429818840481)
XLA Ops:
  0.0 0.7 reshape.6.gain_ref
  0.7 0.0 copy-start
  0.7 0.9 jit_solution_.3.freq_ref
  1.6 0.0 copy-start.1
  1.6 1.4 copy-done.1
  3.0 0.0 copy-start.2
  3.0 1.2 copy-done.2
  4.3 0.0 copy-start.3
  4.3 1.0 copy-done.3
  5.3 0.0 copy-start.4
  5.3 0.7 copy-done.4
  6.0 37.0 %project.1 = (bf16[128,2048]{1,0:T(8,128)(2,1)S(1)}, bf16[1040,128]{1,0:T(8,128)(2,1)S(1)}) custom-call(bf16[512,512]{1,0:T(8,128)(2,1)S(1)} %copy-done.3, f32[8,512]{1,0:T(8,128)S(1)} %reshape.6.gain_ref, f32[64,512]{1,0:T(8,128)S(1)} %jit_solution_.3.freq_ref, s32[1,512]{1,0:T(1,128)S(1)} %bitcast.1, bf16[4096,512]{1,0:T(8,128)(2,1)} %wq.1, ...), custom_call_target="tpu_custom_call" | custom-call | tf_op jit(solution)/shard_map/project/pallas_call | solution.py:226
  43.0 77.5 %attention.1.att = bf16[512,512]{1,0:T(8,128)(2,1)S(1)} custom-call(bf16[128,2048]{1,0:T(8,128)(2,1)S(1)} %get-tuple-element.7.q_ref, s32[1,512]{1,0:T(1,128)S(1)} %bitcast.2, bf16[1040,128]{1,0:T(8,128)(2,1)S(1)} %get-tuple-element.8.own_ref), custom_call_target="tpu_custom_call" | custom-call | tf_op jit(solution)/shard_map/attention/pallas_call | solution.py:611
  120.5 0.0 copy-done
  120.5 35.6 %combine.1 = bf16[512,512]{1,0:T(8,128)(2,1)S(1)} custom-call(bf16[512,512]{1,0:T(8,128)(2,1)S(1)} %attention.1.att, bf16[512,4096]{1,0:T(8,128)(2,1)S(1)} %copy-done), custom_call_target="tpu_custom_call" | custom-call | tf_op jit(solution)/shard_map/combine/pallas_call | solution.py:346
  156.1 0.8 copy.10
Async XLA Ops:
  0.7 119.7 %copy-start = (bf16[512,4096]{1,0:T(8,128)(2,1)S(1)}, bf16[512,4096]{1,0:T(8,128)(2,1)}, u32[]{:S(2)}) copy-start(bf16[512,4096]{1,0:T(8,128)(2,1)} %w_out.1) | copy-start | bytes 12582916
  1.6 1.4 copy-start.1
  3.0 1.2 copy-start.2
  4.3 1.0 copy-start.3
  5.3 0.7 copy-start.4

commit v3 on v2

--- a/solution.py
+++ b/solution.py
@@ -196,8 +196,8 @@
         high = b * cosine[...] + a * sine[...]
         if head < GROUP:
             cols = slice(head * TOK, (head + 1) * TOK)
-            q_out[0:half, cols] = low.astype(jnp.bfloat16)
-            q_out[half:, cols] = high.astype(jnp.bfloat16)
+            q_out[0:half, cols] = (low * SCALE).astype(jnp.bfloat16)
+            q_out[half:, cols] = (high * SCALE).astype(jnp.bfloat16)
         else:
             turned = jnp.concatenate([low, high], axis=0).T
             kv_out[0:TOK, :] = turned.astype(jnp.bfloat16)
@@ -384,76 +384,93 @@
     return jnp.concatenate([block[0:TOK, :], earlier], axis=1)
 
 
-def score(keys, chunk, qaug, logits, tops, causal):
+def score(keys, chunk, slot, qaug, logits, tops, causal):
     cols = slice(chunk * QC, (chunk + 1) * QC)
+    length = keys.shape[0]
     scores = jnp.dot(keys, qaug[:, cols], preferred_element_type=jnp.float32)
     if causal:
         key_at = lax.broadcasted_iota(jnp.int32, (TOK, QC), 0)
         query_at = lax.broadcasted_iota(jnp.int32, (TOK, QC), 1) + (chunk * QC) % TOK
         scores = jnp.where(key_at <= query_at, scores, jnp.float32(PENALTY))
-    logits[chunk % 2] = scores
-    tops[chunk % 2] = jnp.max(scores, axis=0, keepdims=True)
-
-
-def weigh(values, chunk, logits, tops, best, total, acc, first):
+    logits[slot, 0:length] = scores
+    tops[slot] = jnp.max(scores, axis=0, keepdims=True)
+
+
+def weigh(values, chunk, slot, logits, tops, best, acc, first):
     cols = slice(chunk * QC, (chunk + 1) * QC)
-    top = tops[chunk % 2]
+    top = tops[slot]
     if not first:
         old = best[:, cols]
         top = jnp.maximum(old, top)
-    weights = jnp.exp2(logits[chunk % 2] * SCALE - top * SCALE)
-    mass = jnp.sum(weights, axis=0, keepdims=True)
-    out = jnp.dot(values, weights.astype(jnp.bfloat16), preferred_element_type=jnp.float32)
+    weights = jnp.exp2(logits[slot, 0 : values.shape[1]] - top).astype(jnp.bfloat16)
+    out = jnp.dot(values, weights, preferred_element_type=jnp.float32)
     if first:
-        total[:, cols] = mass
         acc[:, cols] = out
     else:
-        shrink = jnp.exp2((old - top) * SCALE)
-        total[:, cols] = total[:, cols] * shrink + mass
-        acc[:, cols] = acc[:, cols] * shrink + out
+        acc[:, cols] = acc[:, cols] * jnp.exp2(old - top) + out
     best[:, cols] = top
 
 
 def attend(blocks, state, first):
-    qaug, logits, tops, best, total, acc = state
+    qaug, logits, tops, best, acc = state
     chunks = ROWS // QC
-    keys = [attend_keys(block) for block in blocks]
-    values = [
-        jnp.concatenate(
-            [block[TOK + 128 * i : TOK + 128 * (i + 1), :] for i in range(TOK // 128)], axis=1
-        )
-        for block in blocks
-    ]
-    score(keys[0], 0, qaug, logits, tops, first)
-    for step in range(len(blocks) * chunks):
-        if step + 1 < len(blocks) * chunks:
-            which, chunk = divmod(step + 1, chunks)
-            score(keys[which], chunk, qaug, logits, tops, first)
-        which, chunk = divmod(step, chunks)
-        weigh(values[which], chunk, logits, tops, best, total, acc, first)
-
-
-def finish(total, acc, out_ref):
+    keys = jnp.concatenate([attend_keys(block) for block in blocks], axis=0)
+    values = jnp.concatenate(
+        [
+            block[TOK + 128 * i : TOK + 128 * (i + 1), :]
+            for block in blocks
+            for i in range(TOK // 128)
+        ],
+        axis=1,
+    )
+    ones = jnp.ones((16, values.shape[1]), jnp.bfloat16)
+    values = jnp.concatenate([values, ones], axis=0)
+    score(keys, 0, 0, qaug, logits, tops, first)
+    for chunk in range(chunks):
+        if chunk + 1 < chunks:
+            score(keys, chunk + 1, (chunk + 1) % 2, qaug, logits, tops, first)
+        weigh(values, chunk, chunk % 2, logits, tops, best, acc, first)
+
+
+def finish(acc, out_ref):
     for head in range(GROUP):
         cols = slice(head * TOK, (head + 1) * TOK)
+        total = acc[HEAD_SIZE : HEAD_SIZE + 1, cols]
         out_ref[:, head * HEAD_SIZE : (head + 1) * HEAD_SIZE] = (
-            (acc[:, cols] / total[:, cols]).T.astype(jnp.bfloat16)
+            (acc[0:HEAD_SIZE, cols] / total).T.astype(jnp.bfloat16)
         )
 
 
 ROLES = 15
 PARTS = ((0, TOK), (TOK, TOK + 16))
+PROGRAM = [
+    (0, [(0, 0), (0, 1), (15, 0), (15, 1)]),
+    (2, [(2, 0), (2, 1), (3, 0), (4, 0)]),
+    (1, [(1, 0), (1, 1), (3, 1), (4, 1)]),
+    (3, []),
+    (4, [(5, 0), (6, 0)]),
+    (5, [(5, 1), (6, 1)]),
+    (6, [(11, 0), (7, 0)]),
+    (9, [(9, 0), (9, 1)]),
+    (8, [(8, 0), (8, 1)]),
+    (11, [(12, 0), (13, 0), (11, 1), (7, 1)]),
+    (7, []),
+    (12, [(12, 1), (13, 1)]),
+    (13, [(10, 0), (10, 1)]),
+    (10, [(14, 0), (14, 1)]),
+    (14, []),
+]
 
 
 def attention_kernel(
     q_ref, doc_ref, own_ref, out_ref,
-    kv, qaug, logits, tops, best, total, acc, ssem, rsem, sibsend, sibrecv,
+    kv, qaug, logits, tops, best, acc, ssem, rsem, sibsend, sibrecv,
 ):
     me = lax.axis_index("cp")
     core = me % 2
     x = (me // 2) % 4
     z = me // 8
-    state = (qaug, logits, tops, best, total, acc)
+    state = (qaug, logits, tops, best, acc)
 
     def at(zz, xx):
         return (zz * 4 + xx) * 2 + core
@@ -496,16 +513,18 @@
         (two, (z + 2) % 4, xm),
         (two, (z + 2) % 4, xp),
         (two, (z + 2) % 4, x2),
+        ((z == 0) & (x < 3), z, xp),
     ]
     slots = [at(zz, xx) for _, zz, xx in roles]
     middle = (x == 1) | (x == 2)
     forwards = {
         0: [(middle, right, (0, 1))],
         3: [(z < 3, ahead, (0, 1)), (always, right, (0, 1)), (always, left, (1, 0))],
-        4: [(x > 0, left, (0, 1)), (x == 3, right, (0, 1))],
+        4: [(x == 3, right, (0, 1))],
         5: [(always, right, (0,))],
         6: [(always, left, (1,))],
         7: [(middle, left, (0, 1))],
+        15: [(always, behind, (0, 1))],
         11: [(always, right, (0, 1)), (always, left, (1, 0))],
         12: [(always, right, (0,))],
         13: [(always, left, (1,))],
@@ -529,7 +548,7 @@
         own.append(plan(z < 3, own_ref, me, half, ahead))
         own.append(plan(z == 0, own_ref, me, half, behind))
         own.append(plan(x < 3, own_ref, me, half, right))
-        own.append(plan(x == 0, own_ref, me, half, left))
+        own.append(plan((x == 0) | (z == 0), own_ref, me, half, left))
     relays = {}
     for role, targets in forwards.items():
         relays[role] = {0: [], 1: []}
@@ -551,41 +570,44 @@
     def _():
         attend([kv.at[sibling]], state, False)
 
-    def serve(role):
+    def serve(role, half):
         slot = slots[role]
-        for half in (0, 1):
-
-            @pl.when(roles[role][0])
-            def _():
-                move(own_ref, slot, half, sibling, ssem.at[0], rsem.at[slot, half]).wait_recv()
+
+        @pl.when(roles[role][0])
+        def _():
+            move(own_ref, slot, half, sibling, ssem.at[0], rsem.at[slot, half]).wait_recv()
+            if role < ROLES:
                 move(
                     kv.at[slot], slot, half, sibling, sibsend.at[role, half], sibrecv.at[role, half]
                 ).start()
 
-            for number in relays.get(role, {0: [], 1: []})[half]:
-                issue(number)
+        for number in relays.get(role, {0: [], 1: []})[half]:
+            issue(number)
 
     @pl.loop(0, ROLES)
     def _(step):
         there = step < 0
         slot = 0 * step
-        for role in range(ROLES):
-
-            @pl.when(step == role)
+        turn = 0 * step
+        for index, (role, services) in enumerate(PROGRAM):
+
+            @pl.when(step == index)
             def _():
-                serve(role)
-
-            there = there | ((step == role) & roles[role][0])
-            slot = jnp.where(step == role, slots[role], slot)
+                for service in services:
+                    serve(*service)
+
+            there = there | ((step == index) & roles[role][0])
+            slot = jnp.where(step == index, slots[role], slot)
+            turn = jnp.where(step == index, role, turn)
 
         @pl.when(there)
         def _():
             twin = slot + 1 - 2 * core
             for half in (0, 1):
-                move(own_ref, twin, half, sibling, sibsend.at[step, half], sibrecv.at[step, half]).wait_recv()
+                move(own_ref, twin, half, sibling, sibsend.at[turn, half], sibrecv.at[turn, half]).wait_recv()
             attend([kv.at[slot], kv.at[twin]], state, False)
 
-    finish(total, acc, out_ref)
+    finish(acc, out_ref)
     for number, (when, source, slot, half, to) in enumerate(sends):
 
         @pl.when(when)
@@ -616,11 +638,10 @@
         scratch_shapes=[
             pltpu.VMEM((32, BLK, 128), jnp.bfloat16),
             pltpu.VMEM((2 * HEAD_SIZE, ROWS), jnp.bfloat16),
-            pltpu.VMEM((2, TOK, QC), jnp.float32),
+            pltpu.VMEM((2, 2 * TOK, QC), jnp.float32),
             pltpu.VMEM((2, 1, QC), jnp.float32),
             pltpu.VMEM((1, ROWS), jnp.float32),
-            pltpu.VMEM((1, ROWS), jnp.float32),
-            pltpu.VMEM((HEAD_SIZE, ROWS), jnp.float32),
+            pltpu.VMEM((HEAD_SIZE + 16, ROWS), jnp.float32),
             pltpu.SemaphoreType.DMA((SENDS,)),
             pltpu.SemaphoreType.DMA((32, 2)),
             pltpu.SemaphoreType.DMA((ROLES + 1, 2)),

time: 158 us -> 139 us (0.88)
  Pallas kernels: 150 us -> 131 us
    pallas_call x1, Pallas kernels: 77.5 us -> 60.3 us  [attention(): pl.pallas_call(attention_kernel, out_shape=jax.ShapeDtypeStruct((TOK, GRO...]
where the time goes in v3:
time: 139 us; the launch traced here: 138 us
  Pallas kernels  131 us (94%)
  local copies, waits for them, and re-layouts  6.77 us (5%)
    pallas_call x1, Pallas kernels, attention(): pl.pallas_call(attention_kernel, out_shape=jax.ShapeDtypeStruct((TOK, GRO...  60.3 us
    pallas_call x1, Pallas kernels, project(): pl.pallas_call(project_kernel, out_shape=(jax.ShapeDtypeStruct((HEAD_SIZE...  37 us
    pallas_call x1, Pallas kernels, combine(): pl.pallas_call(combine_kernel, out_shape=jax.ShapeDtypeStruct((TOK, PIECE...  34.2 us
    unnamed x11, local copies, waits for them, and re-layouts  5.17 us

profile of v3, /device:TPU:224, one launch (start us, length us, event | category | flops | bytes accessed | tf_op | source)
XLA Modules:
  0.0 138.3 jit_solution(16077798880458849624)
XLA Ops:
  0.0 0.7 reshape.6.gain_ref
  0.7 0.0 copy-start
  0.7 0.9 jit_solution_.3.freq_ref
  1.6 0.0 copy-start.1
  1.6 1.4 %copy-done.1 = bf16[4096,128]{1,0:T(8,128)(2,1)S(1)} copy-done((bf16[4096,128]{1,0:T(8,128)(2,1)S(1)}, bf16[4096,128]{1,0:T(8,128)(2,1)}, u32[]{:S(2)}) %copy-start.1) | copy-done | bytes 1048600
  3.0 0.0 copy-start.2
  3.0 1.2 copy-done.2
  4.3 0.0 copy-start.3
  4.3 1.0 copy-done.3
  5.3 0.0 copy-start.4
  5.3 0.7 copy-done.4
  6.0 37.0 %project.1 = (bf16[128,2048]{1,0:T(8,128)(2,1)S(1)}, bf16[1040,128]{1,0:T(8,128)(2,1)S(1)}) custom-call(bf16[512,512]{1,0:T(8,128)(2,1)S(1)} %copy-done.3, f32[8,512]{1,0:T(8,128)S(1)} %reshape.6.gain_ref, f32[64,512]{1,0:T(8,128)S(1)} %jit_solution_.3.freq_ref, s32[1,512]{1,0:T(1,128)S(1)} %bitcast.1, bf16[4096,512]{1,0:T(8,128)(2,1)} %wq.1, ...), custom_call_target="tpu_custom_call" | custom-call | tf_op jit(solution)/shard_map/project/pallas_call | solution.py:226
  43.0 60.3 %attention.1.att = bf16[512,512]{1,0:T(8,128)(2,1)S(1)} custom-call(bf16[128,2048]{1,0:T(8,128)(2,1)S(1)} %get-tuple-element.7.q_ref, s32[1,512]{1,0:T(1,128)S(1)} %bitcast.2, bf16[1040,128]{1,0:T(8,128)(2,1)S(1)} %get-tuple-element.8.own_ref), custom_call_target="tpu_custom_call" | custom-call | tf_op jit(solution)/shard_map/attention/pallas_call | solution.py:633
  103.3 0.0 copy-done
  103.3 34.2 %combine.1 = bf16[512,512]{1,0:T(8,128)(2,1)S(1)} custom-call(bf16[512,512]{1,0:T(8,128)(2,1)S(1)} %attention.1.att, bf16[512,4096]{1,0:T(8,128)(2,1)S(1)} %copy-done), custom_call_target="tpu_custom_call" | custom-call | tf_op jit(solution)/shard_map/combine/pallas_call | solution.py:346
  137.5 0.8 copy.10
Async XLA Ops:
  0.7 102.6 %copy-start = (bf16[512,4096]{1,0:T(8,128)(2,1)S(1)}, bf16[512,4096]{1,0:T(8,128)(2,1)}, u32[]{:S(2)}) copy-start(bf16[512,4096]{1,0:T(8,128)(2,1)} %w_out.1) | copy-start | bytes 12582916
  1.6 1.4 %copy-start.1 = (bf16[4096,128]{1,0:T(8,128)(2,1)S(1)}, bf16[4096,128]{1,0:T(8,128)(2,1)}, u32[]{:S(2)}) copy-start(bf16[4096,128]{1,0:T(8,128)(2,1)} %wk.1) | copy-start | bytes 3145732
  3.0 1.2 copy-start.2
  4.3 1.0 copy-start.3
  5.3 0.7 copy-start.4

commit v4 on v3

--- a/solution.py
+++ b/solution.py
@@ -47,32 +47,19 @@
     return (t + 4) % 8
 
 
-def greet(axis, peers):
-    barrier = pltpu.get_barrier_semaphore()
-    for peer in peers:
-        pl.semaphore_signal(barrier, inc=1, device_id={axis: peer}, device_id_type=MESH)
-    pl.semaphore_wait(barrier, len(peers))
-
-
 def part(chunk):
     return pl.ds(chunk * CR, CR)
 
 
-def project_kernel(
-    h_ref, gain_ref, freq_ref, doc_ref, wq, wk, wv, q_out, kv_out,
-    gath, w, acc, squares, cosine, sine, wsem, ssem, rsem, qssem, qrsem,
+def projection(
+    h_ref, gain_ref, freq_ref, doc_ref, weights, inputs, q_out, kv_out, begin,
+    gath, w, acc, squares, cosine, sine, ssem, rsem, qssem, qrsem,
 ):
     t, up, down, far = tp_places()
     across = other(t)
-    weights = [
-        pltpu.make_async_copy(wq, w.at[:, 0:512], wsem.at[0]),
-        pltpu.make_async_copy(wk, w.at[:, 512:640], wsem.at[1]),
-        pltpu.make_async_copy(wv, w.at[:, 640:768], wsem.at[2]),
-    ]
-    for copy in weights:
-        copy.start()
     peers = [(t + i) % N_TP for i in range(1, N_TP)]
-    greet("tp", peers)
+    for copy in inputs:
+        copy.wait()
     sent = []
 
     def send(source, owner, chunk, to):
@@ -126,7 +113,7 @@
 
     first = lax.axis_index("cp") * TOK
     place = (first + lax.broadcasted_iota(jnp.int32, (HEAD_SIZE // 2, TOK), 1)).astype(jnp.float32)
-    angle = place * freq_ref[...]
+    angle = place * jnp.concatenate([freq_ref[...]] * (TOK // 128), axis=1)
     cosine[...] = jnp.cos(angle)
     sine[...] = jnp.sin(angle)
     for peer in peers:
@@ -146,7 +133,7 @@
         copy.wait()
 
     def use(source, owner, start):
-        gain = gain_ref[pl.ds(owner, 1), :]
+        gain = gain_ref[:, pl.ds(pl.multiple_of(owner * PIECE, PIECE), PIECE)]
         normed = (source[...].astype(jnp.float32) * inverse * gain).astype(jnp.bfloat16)
         rows = pl.ds(pl.multiple_of(owner * PIECE, PIECE), PIECE)
         product = jnp.dot(normed, w[rows, :], preferred_element_type=jnp.float32)
@@ -188,19 +175,15 @@
         use(gath.at[other(side)], other(side), False)
 
     half = HEAD_SIZE // 2
-    for head in range(GROUP + 1):
+
+    def rotated(head):
         raw = acc[:, head * HEAD_SIZE : (head + 1) * HEAD_SIZE].T
-        a = raw[:half]
-        b = raw[half:]
-        low = a * cosine[...] - b * sine[...]
-        high = b * cosine[...] + a * sine[...]
-        if head < GROUP:
-            cols = slice(head * TOK, (head + 1) * TOK)
-            q_out[0:half, cols] = (low * SCALE).astype(jnp.bfloat16)
-            q_out[half:, cols] = (high * SCALE).astype(jnp.bfloat16)
-        else:
-            turned = jnp.concatenate([low, high], axis=0).T
-            kv_out[0:TOK, :] = turned.astype(jnp.bfloat16)
+        low = raw[:half] * cosine[...] - raw[half:] * sine[...]
+        high = raw[half:] * cosine[...] + raw[:half] * sine[...]
+        return low, high
+
+    low, high = rotated(GROUP)
+    kv_out[0:TOK, :] = jnp.concatenate([low, high], axis=0).T.astype(jnp.bfloat16)
     value = acc[:, (GROUP + 1) * HEAD_SIZE :].T.astype(jnp.bfloat16)
     for i in range(TOK // 128):
         kv_out[TOK + 128 * i : TOK + 128 * (i + 1), :] = value[:, 128 * i : 128 * (i + 1)]
@@ -213,58 +196,20 @@
             (lane == d) & (row == 0), count // 16, jnp.where((lane == d) & (row == 1), count % 16, tail)
         )
     kv_out[2 * TOK :, :] = tail.astype(jnp.float32).astype(jnp.bfloat16)
-    for copy in sent + told:
-        copy.wait_send()
-
-
-def project(hidden, norm_gain, w_query, w_key, w_value, doc_ids):
-    vmem = pl.BlockSpec(memory_space=pltpu.VMEM)
-    hbm = pl.BlockSpec(memory_space=pl.ANY)
-    powers = -np.arange(HEAD_SIZE // 2, dtype=np.float32) * np.float32(2.0) / HEAD_SIZE
-    freqs = (np.float64(rope_base) ** powers.astype(np.float64)).astype(np.float32)
-    freqs = jnp.asarray(np.broadcast_to(freqs[:, None], (HEAD_SIZE // 2, TOK)))
-    return pl.pallas_call(
-        project_kernel,
-        out_shape=(
-            jax.ShapeDtypeStruct((HEAD_SIZE, ROWS), jnp.bfloat16),
-            jax.ShapeDtypeStruct((BLK, 128), jnp.bfloat16),
-        ),
-        in_specs=[vmem] * 4 + [hbm] * 3,
-        out_specs=(vmem, vmem),
-        scratch_shapes=[
-            pltpu.VMEM((N_TP, TOK, PIECE), jnp.bfloat16),
-            pltpu.VMEM((WIDTH, 768), jnp.bfloat16),
-            pltpu.VMEM((TOK, 768), jnp.float32),
-            pltpu.VMEM((N_TP, 8, TOK), jnp.float32),
-            pltpu.VMEM((HEAD_SIZE // 2, TOK), jnp.float32),
-            pltpu.VMEM((HEAD_SIZE // 2, TOK), jnp.float32),
-            pltpu.SemaphoreType.DMA((3,)),
-            pltpu.SemaphoreType.DMA((28,)),
-            pltpu.SemaphoreType.DMA((N_TP, CH)),
-            pltpu.SemaphoreType.DMA((N_TP - 1,)),
-            pltpu.SemaphoreType.DMA((N_TP,)),
-        ],
-        compiler_params=pltpu.CompilerParams(
-            collective_id=0, has_side_effects=True, vmem_limit_bytes=48 * 2**20
-        ),
-        name="project",
-    )(hidden, norm_gain.reshape(N_TP, PIECE), freqs, doc_ids, w_query, w_key, w_value)
-
-
-def combine_kernel(
-    att, w_out, out_ref,
-    w, terms, sums, across_in, side_in, half_in, side_end, across_end,
-    wsem, ssem, rsem,
+    begin()
+    for head in range(GROUP):
+        low, high = rotated(head)
+        cols = slice(head * TOK, (head + 1) * TOK)
+        q_out[0:half, cols] = (low * SCALE).astype(jnp.bfloat16)
+        q_out[half:HEAD_SIZE, cols] = (high * SCALE).astype(jnp.bfloat16)
+    return sent + told
+
+
+def combination(
+    att, out_ref, weights, w, terms, sums, across_in, side_in, half_in, side_end, across_end, ssem, rsem,
 ):
     t, up, down, far = tp_places()
     across = other(t)
-    order = [other(far), other(up), other(down), far, across, up, down, t]
-    weights = []
-    for i, owner in enumerate(order):
-        cols = pl.ds(pl.multiple_of(owner * PIECE, PIECE), PIECE)
-        weights.append(pltpu.make_async_copy(w_out.at[:, cols], w.at[i], wsem.at[i]))
-        weights[-1].start()
-    greet("tp", (up, down, across))
     sent = []
 
     def send(source, target, number, to):
@@ -336,40 +281,10 @@
         total = total + arrived(side_end.at[DOWN, part(chunk)], 20 + chunk)
         total = total + arrived(side_end.at[UP, part(chunk)], 24 + chunk)
         out_ref[part(chunk), :] = total.astype(jnp.bfloat16)
-    for copy in sent:
-        copy.wait_send()
-
-
-def combine(attended, w_out):
-    vmem = pl.BlockSpec(memory_space=pltpu.VMEM)
-    hbm = pl.BlockSpec(memory_space=pl.ANY)
-    return pl.pallas_call(
-        combine_kernel,
-        out_shape=jax.ShapeDtypeStruct((TOK, PIECE), jnp.bfloat16),
-        in_specs=[vmem, hbm],
-        out_specs=vmem,
-        scratch_shapes=[
-            pltpu.VMEM((N_TP, PIECE, PIECE), jnp.bfloat16),
-            pltpu.VMEM((N_TP, TOK, PIECE), jnp.bfloat16),
-            pltpu.VMEM((4, TOK, PIECE), jnp.bfloat16),
-            pltpu.VMEM((TOK, PIECE), jnp.bfloat16),
-            pltpu.VMEM((2, TOK, PIECE), jnp.bfloat16),
-            pltpu.VMEM((2, TOK // 2, PIECE), jnp.bfloat16),
-            pltpu.VMEM((2, TOK, PIECE), jnp.bfloat16),
-            pltpu.VMEM((TOK, PIECE), jnp.bfloat16),
-            pltpu.SemaphoreType.DMA((N_TP,)),
-            pltpu.SemaphoreType.DMA((28,)),
-            pltpu.SemaphoreType.DMA((28,)),
-        ],
-        compiler_params=pltpu.CompilerParams(
-            collective_id=1, has_side_effects=True, vmem_limit_bytes=40 * 2**20
-        ),
-        name="combine",
-    )(attended, w_out)
-
-
-def augment_queries(q_ref, doc_ref, qaug):
-    qaug[0:HEAD_SIZE, :] = q_ref[...]
+    return sent
+
+
+def augment_queries(doc_ref, qaug):
     row = lax.broadcasted_iota(jnp.int32, (HEAD_SIZE, TOK), 0)
     hot = jnp.where(row == doc_ref[...], PENALTY, 0.0).astype(jnp.bfloat16)
     for head in range(GROUP):
@@ -453,7 +368,7 @@
     (6, [(11, 0), (7, 0)]),
     (9, [(9, 0), (9, 1)]),
     (8, [(8, 0), (8, 1)]),
-    (11, [(12, 0), (13, 0), (11, 1), (7, 1)]),
+    (11, [(11, 1), (12, 0), (13, 0), (7, 1)]),
     (7, []),
     (12, [(12, 1), (13, 1)]),
     (13, [(10, 0), (10, 1)]),
@@ -462,9 +377,8 @@
 ]
 
 
-def attention_kernel(
-    q_ref, doc_ref, own_ref, out_ref,
-    kv, qaug, logits, tops, best, acc, ssem, rsem, sibsend, sibrecv,
+def attention(
+    doc_ref, own_ref, out_ref, kv, qaug, logits, tops, best, acc, ssem, rsem, sibsend, sibrecv,
 ):
     me = lax.axis_index("cp")
     core = me % 2
@@ -480,7 +394,6 @@
     ahead = at((z + 1) % 4, x)
     behind = at((z + 3) % 4, x)
     sibling = me + 1 - 2 * core
-    greet("cp", (right, left, ahead, behind, sibling))
 
     def move(source, slot, half, to, send_sem, recv_sem):
         rows = pl.ds(*PARTS[half])
@@ -557,18 +470,11 @@
                 number = plan(roles[role][0] & when, kv.at[slots[role]], slots[role], half, to)
                 relays[role][half].append(number)
 
-    for half in (0, 1):
-        move(own_ref, me, half, sibling, sibsend.at[ROLES, half], sibrecv.at[ROLES, half]).start()
-    for number in own:
-        issue(number)
-    augment_queries(q_ref, doc_ref, qaug)
-    attend([own_ref], state, True)
-    for half in (0, 1):
-        move(own_ref, sibling, half, sibling, sibsend.at[ROLES, half], sibrecv.at[ROLES, half]).wait_recv()
-
-    @pl.when(core == 1)
-    def _():
-        attend([kv.at[sibling]], state, False)
+    def begin():
+        for number in own:
+            issue(number)
+        for half in (0, 1):
+            move(own_ref, me, half, sibling, sibsend.at[ROLES, half], sibrecv.at[ROLES, half]).start()
 
     def serve(role, half):
         slot = slots[role]
@@ -584,81 +490,184 @@
         for number in relays.get(role, {0: [], 1: []})[half]:
             issue(number)
 
-    @pl.loop(0, ROLES)
-    def _(step):
-        there = step < 0
-        slot = 0 * step
-        turn = 0 * step
-        for index, (role, services) in enumerate(PROGRAM):
-
-            @pl.when(step == index)
+    def run():
+        augment_queries(doc_ref, qaug)
+        attend([own_ref], state, True)
+        for half in (0, 1):
+            move(own_ref, sibling, half, sibling, sibsend.at[ROLES, half], sibrecv.at[ROLES, half]).wait_recv()
+
+        @pl.when(core == 1)
+        def _():
+            attend([kv.at[sibling]], state, False)
+
+        @pl.loop(0, ROLES)
+        def _(step):
+            there = step < 0
+            slot = 0 * step
+            turn = 0 * step
+            for index, (role, services) in enumerate(PROGRAM):
+
+                @pl.when(step == index)
+                def _():
+                    for service in services:
+                        serve(*service)
+
+                there = there | ((step == index) & roles[role][0])
+                slot = jnp.where(step == index, slots[role], slot)
+                turn = jnp.where(step == index, role, turn)
+
+            @pl.when(there)
             def _():
-                for service in services:
-                    serve(*service)
-
-            there = there | ((step == index) & roles[role][0])
-            slot = jnp.where(step == index, slots[role], slot)
-            turn = jnp.where(step == index, role, turn)
-
-        @pl.when(there)
-        def _():
-            twin = slot + 1 - 2 * core
+                twin = slot + 1 - 2 * core
+                for half in (0, 1):
+                    move(own_ref, twin, half, sibling, sibsend.at[turn, half], sibrecv.at[turn, half]).wait_recv()
+                attend([kv.at[slot], kv.at[twin]], state, False)
+
+        finish(acc, out_ref)
+
+    def drain():
+        for number, (when, source, slot, half, to) in enumerate(sends):
+
+            @pl.when(when)
+            def _():
+                move(source, slot, half, to, ssem.at[number], rsem.at[slot, half]).wait_send()
+
+        for role in range(ROLES + 1):
+            present, slot = (always, me) if role == ROLES else (roles[role][0], slots[role])
             for half in (0, 1):
-                move(own_ref, twin, half, sibling, sibsend.at[turn, half], sibrecv.at[turn, half]).wait_recv()
-            attend([kv.at[slot], kv.at[twin]], state, False)
-
-    finish(acc, out_ref)
-    for number, (when, source, slot, half, to) in enumerate(sends):
-
-        @pl.when(when)
-        def _():
-            move(source, slot, half, to, ssem.at[number], rsem.at[slot, half]).wait_send()
-
-    for role in range(ROLES + 1):
-        present, slot = (always, me) if role == ROLES else (roles[role][0], slots[role])
-        for half in (0, 1):
-
-            @pl.when(present)
-            def _():
-                move(
-                    own_ref, slot, half, sibling, sibsend.at[role, half], sibrecv.at[role, half]
-                ).wait_send()
+
+                @pl.when(present)
+                def _():
+                    move(
+                        own_ref, slot, half, sibling, sibsend.at[role, half], sibrecv.at[role, half]
+                    ).wait_send()
+
+    return begin, run, drain
 
 
 SENDS = 30
-
-
-def attention(queries, docs, block):
-    vmem = pl.BlockSpec(memory_space=pltpu.VMEM)
+BF16, F32 = jnp.bfloat16, jnp.float32
+
+
+def fused_kernel(
+    h_hbm, gain_hbm, freq_hbm, doc_hbm, wq, wk, wv, w_out, out_ref,
+    gath, w, pacc, squares, cosine, sine, gain_ref, freq_ref, doc_ref, insem, pssem, prsem, qssem, qrsem,
+    own, kv, qaug, logits, tops, best, acc, assem, arsem, sibsend, sibrecv, att,
+    wo, terms, sums, across_in, side_in, half_in, side_end, across_end, wosem, cssem, crsem,
+):
+    t, up, down, far = tp_places()
+    across = other(t)
+    me = lax.axis_index("cp")
+    h_ref = gath.at[t]
+    inputs = [
+        pltpu.make_async_copy(h_hbm, h_ref, insem.at[0]),
+        pltpu.make_async_copy(freq_hbm, freq_ref, insem.at[1]),
+        pltpu.make_async_copy(gain_hbm, gain_ref, insem.at[2]),
+        pltpu.make_async_copy(doc_hbm, doc_ref, insem.at[3]),
+    ]
+    weights = [
+        pltpu.make_async_copy(wq, w.at[:, 0:512], insem.at[4]),
+        pltpu.make_async_copy(wk, w.at[:, 512:640], insem.at[5]),
+        pltpu.make_async_copy(wv, w.at[:, 640:768], insem.at[6]),
+    ]
+    order = [other(far), other(up), other(down), far, across, up, down, t]
+    late = []
+    for i, owner in enumerate(order):
+        cols = pl.ds(pl.multiple_of(owner * PIECE, PIECE), PIECE)
+        late.append(pltpu.make_async_copy(w_out.at[:, cols], wo.at[i], wosem.at[i]))
+    for copy in inputs + weights + late:
+        copy.start()
+    core = me % 2
+    column = (me // 2) % 4
+    row = me // 8
+    barrier = pltpu.get_barrier_semaphore()
+    around = [
+        me - me % 8 + (me + 2) % 8,
+        me - me % 8 + (me + 6) % 8,
+        (me + 8) % 32,
+        (me + 24) % 32,
+        me + 1 - 2 * core,
+    ]
+    for i in range(1, N_TP):
+        pl.semaphore_signal(barrier, inc=1, device_id={"tp": (t + i) % N_TP}, device_id_type=MESH)
+    for peer in around:
+        pl.semaphore_signal(barrier, inc=1, device_id={"cp": peer}, device_id_type=MESH)
+    pl.semaphore_wait(barrier, N_TP - 1 + len(around))
+
+    begin, run, drain = attention(
+        doc_ref, own, att, kv, qaug, logits, tops, best, acc, assem, arsem, sibsend, sibrecv
+    )
+    sent = projection(
+        h_ref, gain_ref, freq_ref, doc_ref, weights, inputs, qaug, own, begin,
+        gath, w, pacc, squares, cosine, sine, pssem, prsem, qssem, qrsem,
+    )
+    run()
+    sent += combination(
+        att, out_ref, late, wo, terms, sums, across_in, side_in, half_in, side_end, across_end, cssem, crsem
+    )
+    drain()
+    for copy in sent:
+        copy.wait_send()
+
+
+def sublayer(hidden, norm_gain, w_query, w_key, w_value, w_out, doc_ids):
+    hbm = pl.BlockSpec(memory_space=pl.ANY)
+    powers = -np.arange(HEAD_SIZE // 2, dtype=np.float32) * np.float32(2.0) / HEAD_SIZE
+    freqs = (np.float64(rope_base) ** powers.astype(np.float64)).astype(np.float32)
+    freqs = jnp.asarray(np.broadcast_to(freqs[:, None], (HEAD_SIZE // 2, 128)))
+    dma = pltpu.SemaphoreType.DMA
     return pl.pallas_call(
-        attention_kernel,
-        out_shape=jax.ShapeDtypeStruct((TOK, GROUP * HEAD_SIZE), jnp.bfloat16),
-        in_specs=[vmem] * 3,
-        out_specs=vmem,
+        fused_kernel,
+        out_shape=jax.ShapeDtypeStruct((TOK, PIECE), BF16),
+        in_specs=[hbm] * 8,
+        out_specs=pl.BlockSpec(memory_space=pltpu.VMEM),
         scratch_shapes=[
-            pltpu.VMEM((32, BLK, 128), jnp.bfloat16),
-            pltpu.VMEM((2 * HEAD_SIZE, ROWS), jnp.bfloat16),
-            pltpu.VMEM((2, 2 * TOK, QC), jnp.float32),
-            pltpu.VMEM((2, 1, QC), jnp.float32),
-            pltpu.VMEM((1, ROWS), jnp.float32),
-            pltpu.VMEM((HEAD_SIZE + 16, ROWS), jnp.float32),
-            pltpu.SemaphoreType.DMA((SENDS,)),
-            pltpu.SemaphoreType.DMA((32, 2)),
-            pltpu.SemaphoreType.DMA((ROLES + 1, 2)),
-            pltpu.SemaphoreType.DMA((ROLES + 1, 2)),
+            pltpu.VMEM((N_TP, TOK, PIECE), BF16),
+            pltpu.VMEM((WIDTH, 768), BF16),
+            pltpu.VMEM((TOK, 768), F32),
+            pltpu.VMEM((N_TP, 8, TOK), F32),
+            pltpu.VMEM((HEAD_SIZE // 2, TOK), F32),
+            pltpu.VMEM((HEAD_SIZE // 2, TOK), F32),
+            pltpu.VMEM((1, WIDTH), F32),
+            pltpu.VMEM((HEAD_SIZE // 2, 128), F32),
+            pltpu.VMEM((1, TOK), jnp.int32),
+            dma((7,)),
+            dma((28,)),
+            dma((N_TP, CH)),
+            dma((N_TP - 1,)),
+            dma((N_TP,)),
+            pltpu.VMEM((BLK, 128), BF16),
+            pltpu.VMEM((32, BLK, 128), BF16),
+            pltpu.VMEM((2 * HEAD_SIZE, ROWS), BF16),
+            pltpu.VMEM((2, 2 * TOK, QC), F32),
+            pltpu.VMEM((2, 1, QC), F32),
+            pltpu.VMEM((1, ROWS), F32),
+            pltpu.VMEM((HEAD_SIZE + 16, ROWS), F32),
+            dma((SENDS,)),
+            dma((32, 2)),
+            dma((ROLES + 1, 2)),
+            dma((ROLES + 1, 2)),
+            pltpu.VMEM((TOK, GROUP * HEAD_SIZE), BF16),
+            pltpu.VMEM((N_TP, PIECE, PIECE), BF16),
+            pltpu.VMEM((N_TP, TOK, PIECE), BF16),
+            pltpu.VMEM((4, TOK, PIECE), BF16),
+            pltpu.VMEM((TOK, PIECE), BF16),
+            pltpu.VMEM((2, TOK, PIECE), BF16),
+            pltpu.VMEM((2, TOK // 2, PIECE), BF16),
+            pltpu.VMEM((2, TOK, PIECE), BF16),
+            pltpu.VMEM((TOK, PIECE), BF16),
+            dma((N_TP,)),
+            dma((28,)),
+            dma((28,)),
         ],
         compiler_params=pltpu.CompilerParams(
-            collective_id=2, has_side_effects=True, vmem_limit_bytes=40 * 2**20
+            collective_id=0, has_side_effects=True, vmem_limit_bytes=63 * 2**20
         ),
-        name="attention",
-    )(queries, docs, block)
-
-
-def shards(hidden, norm_gain, w_query, w_key, w_value, w_out, doc_ids):
-    docs = doc_ids.reshape(1, TOK)
-    queries, block = project(hidden, norm_gain, w_query, w_key, w_value, docs)
-    attended = attention(queries, docs, block)
-    return combine(attended, w_out)
+        name="sublayer",
+    )(
+        hidden, norm_gain.reshape(1, WIDTH), freqs, doc_ids.reshape(1, TOK),
+        w_query, w_key, w_value, w_out,
+    )
 
 
 def solution(mesh):
@@ -672,5 +681,5 @@
         P("cp"),
     )
     return jax.shard_map(
-        shards, mesh=mesh, in_specs=in_specs, out_specs=P("cp", "tp"), check_vma=False
+        sublayer, mesh=mesh, in_specs=in_specs, out_specs=P("cp", "tp"), check_vma=False
     )

time: 139 us -> 131 us (0.942)
  local copies, waits for them, and re-layouts: 6.77 us -> 3.21 us
  Pallas kernels: 131 us -> 128 us
    pallas_call x3 -> x1, Pallas kernels: 131 us -> 128 us  [sublayer(): pl.pallas_call(fused_kernel, out_shape=jax.ShapeDtypeStruct((TOK, PIECE),...]
    unnamed x11 -> x1, local copies, waits for them, and re-layouts: 5.17 us -> 1.87 us
where the time goes in v4:
time: 131 us
  Pallas kernels  128 us (98%)
  local copies, waits for them, and re-layouts  3.21 us (2%)
    pallas_call x1, Pallas kernels, sublayer(): pl.pallas_call(fused_kernel, out_shape=jax.ShapeDtypeStruct((TOK, PIECE),...  128 us

profile of v4, /device:TPU:224, one launch (start us, length us, event | category | flops | bytes accessed | tf_op | source)
XLA Modules:
  0.0 131.1 jit_solution(7213482791030903290)
XLA Ops:
  0.0 1.3 %jit_solution_.3.freq_hbm = f32[64,128]{1,0:T(8,128)} broadcast(f32[64]{0:T(128)} %constant.2.clone), dimensions={0} | broadcast | bytes 33024 | tf_op jit(solution)
  1.3 127.9 %sublayer.1 = bf16[512,512]{1,0:T(8,128)(2,1)} custom-call(bf16[512,512]{1,0:T(8,128)(2,1)} %h_hbm.1, f32[1,4096]{1,0:T(1,128)} %bitcast.2, f32[64,128]{1,0:T(8,128)} %jit_solution_.3.freq_hbm, s32[1,512]{1,0:T(1,128)} %bitcast.3, bf16[4096,512]{1,0:T(8,128)(2,1)} %wq.1, bf16[4096,128]{1,0:T(8,128)(2,1)} %wk.1, bf16[4096,128]{1,0:T(8,128)(2,1)} %wv.1, ...), custom_call_target="tpu_custom_call" | custom-call | tf_op jit(solution)/shard_map/sublayer/pallas_call | solution.py:619
  129.2 1.9 %copy.10 = bf16[512,512]{1,0:T(8,128)(2,1)} copy(bf16[512,512]{1,0:T(8,128)(2,1)} %sublayer.1) | data formatting | bytes 1048576

commit v5 on v4

--- a/solution.py
+++ b/solution.py
@@ -30,6 +30,7 @@
 N_TP = 8
 CH = 4
 CR = TOK // CH
+HALF = TOK // 2
 MESH = pl.DeviceIdType.MESH
 
 
@@ -52,7 +53,7 @@
 
 
 def projection(
-    h_ref, gain_ref, freq_ref, doc_ref, weights, inputs, q_out, kv_out, begin,
+    h_ref, gain_ref, freq_ref, doc_ref, weights, inputs, q_out, kv_out, begin, serve,
     gath, w, acc, squares, cosine, sine, ssem, rsem, qssem, qrsem,
 ):
     t, up, down, far = tp_places()
@@ -84,15 +85,15 @@
             device_id_type=MESH,
         ).wait_recv()
 
-    upward = (0, 1, 2, 3)
-    downward = (2, 3, 0, 1)
-
-    def send_own(i):
-        send(h_ref.at[part(upward[i])], t, upward[i], up)
-        send(h_ref.at[part(downward[i])], t, downward[i], down)
-        send(h_ref.at[part(upward[i])], t, upward[i], across)
-
-    send_own(0)
+    def own(chunk, to):
+        send(h_ref.at[part(chunk)], t, chunk, to)
+
+    def relay(owner, chunk, to):
+        send(gath.at[owner, part(chunk)], owner, chunk, to)
+
+    own(0, up)
+    own(1, down)
+    own(0, across)
     mine = h_ref[...].astype(jnp.float32)
     mass = jnp.sum(mine * mine, axis=1, keepdims=True)
     squares[t] = jnp.broadcast_to(mass, (TOK, 128)).T[0:8]
@@ -108,8 +109,10 @@
         )
         copy.start()
         told.append(copy)
-    for i in range(1, CH):
-        send_own(i)
+    own(1, up)
+    own(0, down)
+    own(1, across)
+    own(2, across)
 
     first = lax.axis_index("cp") * TOK
     place = (first + lax.broadcasted_iota(jnp.int32, (HEAD_SIZE // 2, TOK), 1)).astype(jnp.float32)
@@ -132,61 +135,59 @@
     for copy in weights:
         copy.wait()
 
-    def use(source, owner, start):
+    def use(owner, second, start=False):
+        rows = slice(second * HALF, (second + 1) * HALF)
         gain = gain_ref[:, pl.ds(pl.multiple_of(owner * PIECE, PIECE), PIECE)]
-        normed = (source[...].astype(jnp.float32) * inverse * gain).astype(jnp.bfloat16)
-        rows = pl.ds(pl.multiple_of(owner * PIECE, PIECE), PIECE)
-        product = jnp.dot(normed, w[rows, :], preferred_element_type=jnp.float32)
+        wide = gath[owner, rows].astype(jnp.float32)
+        normed = (wide * inverse[rows] * gain).astype(jnp.bfloat16)
+        deep = pl.ds(pl.multiple_of(owner * PIECE, PIECE), PIECE)
+        product = jnp.dot(normed, w[deep, :], preferred_element_type=jnp.float32)
         if start:
-            acc[...] = product
+            acc[rows, :] = product
         else:
-            acc[...] += product
-
-    use(h_ref, t, True)
-    for i in range(CH):
-        arrived(down, upward[i])
-        if i < 2:
-            send(gath.at[down, part(upward[i])], down, upward[i], up)
-        arrived(up, downward[i])
-        if i < 2:
-            send(gath.at[up, part(downward[i])], up, downward[i], down)
-        arrived(across, upward[i])
-        if i == 1:
-            for chunk in (0, 1):
-                send(gath.at[across, part(chunk)], across, chunk, up)
-                send(gath.at[across, part(chunk)], across, chunk, down)
-        if i > 1:
-            send(gath.at[across, part(i)], across, i, up)
-            send(gath.at[across, part(i)], across, i, down)
-    use(gath.at[up], up, False)
-    use(gath.at[down], down, False)
-    for i in range(2):
-        for chunk in (upward[i], downward[i]):
-            arrived(far, chunk)
-            send(gath.at[far, part(chunk)], far, chunk, across)
-    use(gath.at[across], across, False)
-    use(gath.at[far], far, False)
-    for chunk in (0, 2, 1, 3):
-        arrived(other(far), chunk)
-    use(gath.at[other(far)], other(far), False)
-    for side in (up, down):
-        for chunk in range(CH):
-            arrived(other(side), chunk)
-        use(gath.at[other(side)], other(side), False)
+            acc[rows, :] += product
 
     half = HEAD_SIZE // 2
 
-    def rotated(head):
-        raw = acc[:, head * HEAD_SIZE : (head + 1) * HEAD_SIZE].T
-        low = raw[:half] * cosine[...] - raw[half:] * sine[...]
-        high = raw[half:] * cosine[...] + raw[:half] * sine[...]
+    def rotated(head, second):
+        rows = slice(second * HALF, (second + 1) * HALF)
+        raw = acc[rows, head * HEAD_SIZE : (head + 1) * HEAD_SIZE].T
+        low = raw[:half] * cosine[:, rows] - raw[half:] * sine[:, rows]
+        high = raw[half:] * cosine[:, rows] + raw[:half] * sine[:, rows]
         return low, high
 
-    low, high = rotated(GROUP)
-    kv_out[0:TOK, :] = jnp.concatenate([low, high], axis=0).T.astype(jnp.bfloat16)
-    value = acc[:, (GROUP + 1) * HEAD_SIZE :].T.astype(jnp.bfloat16)
-    for i in range(TOK // 128):
-        kv_out[TOK + 128 * i : TOK + 128 * (i + 1), :] = value[:, 128 * i : 128 * (i + 1)]
+    def finish_pairs(second):
+        base = second * TOK
+        rows = slice(second * HALF, (second + 1) * HALF)
+        low, high = rotated(GROUP, second)
+        turned = jnp.concatenate([low, high], axis=0).T
+        kv_out[base : base + HALF, :] = turned.astype(jnp.bfloat16)
+        value = acc[rows, (GROUP + 1) * HEAD_SIZE :].T.astype(jnp.bfloat16)
+        for i in range(HALF // 128):
+            at = base + HALF + 128 * i
+            kv_out[at : at + 128, :] = value[:, 128 * i : 128 * (i + 1)]
+
+    def finish_queries(second):
+        for head in range(GROUP):
+            low, high = rotated(head, second)
+            cols = slice(head * TOK + second * HALF, head * TOK + (second + 1) * HALF)
+            q_out[0:half, cols] = (low * SCALE).astype(jnp.bfloat16)
+            q_out[half:HEAD_SIZE, cols] = (high * SCALE).astype(jnp.bfloat16)
+
+    use(t, 0, True)
+    arrived(down, 0)
+    relay(down, 0, up)
+    arrived(up, 1)
+    relay(up, 1, down)
+    for chunk in (0, 1):
+        arrived(across, chunk)
+        relay(across, chunk, up)
+        relay(across, chunk, down)
+    own(2, up)
+    own(3, down)
+    own(3, up)
+    own(2, down)
+    use(t, 1, True)
     lane = lax.broadcasted_iota(jnp.int32, (16, 128), 1)
     row = lax.broadcasted_iota(jnp.int32, (16, 128), 0)
     tail = jnp.zeros((16, 128), jnp.int32)
@@ -196,12 +197,57 @@
             (lane == d) & (row == 0), count // 16, jnp.where((lane == d) & (row == 1), count % 16, tail)
         )
     kv_out[2 * TOK :, :] = tail.astype(jnp.float32).astype(jnp.bfloat16)
-    begin()
-    for head in range(GROUP):
-        low, high = rotated(head)
-        cols = slice(head * TOK, (head + 1) * TOK)
-        q_out[0:half, cols] = (low * SCALE).astype(jnp.bfloat16)
-        q_out[half:HEAD_SIZE, cols] = (high * SCALE).astype(jnp.bfloat16)
+    arrived(down, 1)
+    arrived(up, 0)
+    use(up, 0)
+    use(down, 0)
+    arrived(far, 0)
+    relay(far, 0, across)
+    arrived(far, 1)
+    relay(far, 1, across)
+    own(3, across)
+    use(across, 0)
+    use(far, 0)
+    for side in (up, down):
+        arrived(other(side), 0)
+        arrived(other(side), 1)
+        use(other(side), 0)
+    arrived(other(far), 0)
+    arrived(other(far), 1)
+    use(other(far), 0)
+    finish_pairs(0)
+    begin(0)
+    arrived(down, 2)
+    relay(down, 2, up)
+    arrived(up, 3)
+    relay(up, 3, down)
+    for chunk in (2, 3):
+        arrived(across, chunk)
+        relay(across, chunk, up)
+        relay(across, chunk, down)
+    finish_queries(0)
+    arrived(down, 3)
+    arrived(up, 2)
+    use(up, 1)
+    use(down, 1)
+    arrived(far, 2)
+    relay(far, 2, across)
+    arrived(far, 3)
+    relay(far, 3, across)
+    use(across, 1)
+    for service in EARLY:
+        serve(*service)
+    use(far, 1)
+    for side in (up, down):
+        arrived(other(side), 2)
+        arrived(other(side), 3)
+        use(other(side), 1)
+    arrived(other(far), 2)
+    arrived(other(far), 3)
+    use(other(far), 1)
+    finish_pairs(1)
+    begin(1)
+    finish_queries(1)
     return sent + told
 
 
@@ -296,7 +342,8 @@
     below = counts[0:1] * 16.0 + counts[1:2]
     row = lax.broadcasted_iota(jnp.int32, (TOK, HEAD_SIZE), 0).astype(jnp.float32)
     earlier = jnp.where(row < below, 1.0, 0.0).astype(jnp.bfloat16)
-    return jnp.concatenate([block[0:TOK, :], earlier], axis=1)
+    keys = jnp.concatenate([block[0:HALF, :], block[TOK : TOK + HALF, :]], axis=0)
+    return jnp.concatenate([keys, earlier], axis=1)
 
 
 def score(keys, chunk, slot, qaug, logits, tops, causal):
@@ -332,9 +379,9 @@
     keys = jnp.concatenate([attend_keys(block) for block in blocks], axis=0)
     values = jnp.concatenate(
         [
-            block[TOK + 128 * i : TOK + 128 * (i + 1), :]
+            block[at : at + 128, :]
             for block in blocks
-            for i in range(TOK // 128)
+            for at in (HALF, HALF + 128, TOK + HALF, TOK + HALF + 128)
         ],
         axis=1,
     )
@@ -358,21 +405,22 @@
 
 ROLES = 15
 PARTS = ((0, TOK), (TOK, TOK + 16))
+EARLY = [(0, 0), (2, 0), (15, 0), (3, 0), (4, 0), (1, 0)]
 PROGRAM = [
-    (0, [(0, 0), (0, 1), (15, 0), (15, 1)]),
-    (2, [(2, 0), (2, 1), (3, 0), (4, 0)]),
-    (1, [(1, 0), (1, 1), (3, 1), (4, 1)]),
-    (3, []),
-    (4, [(5, 0), (6, 0)]),
-    (5, [(5, 1), (6, 1)]),
-    (6, [(11, 0), (7, 0)]),
-    (9, [(9, 0), (9, 1)]),
-    (8, [(8, 0), (8, 1)]),
-    (11, [(11, 1), (12, 0), (13, 0), (7, 1)]),
-    (7, []),
-    (12, [(12, 1), (13, 1)]),
-    (13, [(10, 0), (10, 1)]),
-    (10, [(14, 0), (14, 1)]),
+    (0, [(5, 0), (6, 0), (11, 0), (7, 0), (0, 1), (15, 1)]),
+    (2, [(2, 1), (9, 0)]),
+    (1, [(3, 1), (4, 1), (1, 1), (12, 0), (13, 0)]),
+    (3, [(8, 0), (10, 0)]),
+    (4, [(5, 1), (6, 1), (14, 0)]),
+    (5, [(11, 1), (7, 1)]),
+    (6, [(9, 1)]),
+    (9, [(8, 1)]),
+    (8, []),
+    (11, [(12, 1), (13, 1)]),
+    (7, [(10, 1)]),
+    (12, [(14, 1)]),
+    (13, []),
+    (10, []),
     (14, []),
 ]
 
@@ -456,12 +504,12 @@
         def _():
             move(source, slot, half, to, ssem.at[number], rsem.at[slot, half]).start()
 
-    own = []
+    own = [[], []]
     for half in (0, 1):
-        own.append(plan(z < 3, own_ref, me, half, ahead))
-        own.append(plan(z == 0, own_ref, me, half, behind))
-        own.append(plan(x < 3, own_ref, me, half, right))
-        own.append(plan((x == 0) | (z == 0), own_ref, me, half, left))
+        own[half].append(plan(z < 3, own_ref, me, half, ahead))
+        own[half].append(plan(z == 0, own_ref, me, half, behind))
+        own[half].append(plan(x < 3, own_ref, me, half, right))
+        own[half].append(plan((x == 0) | (z == 0), own_ref, me, half, left))
     relays = {}
     for role, targets in forwards.items():
         relays[role] = {0: [], 1: []}
@@ -470,11 +518,10 @@
                 number = plan(roles[role][0] & when, kv.at[slots[role]], slots[role], half, to)
                 relays[role][half].append(number)
 
-    def begin():
-        for number in own:
+    def begin(half):
+        for number in own[half]:
             issue(number)
-        for half in (0, 1):
-            move(own_ref, me, half, sibling, sibsend.at[ROLES, half], sibrecv.at[ROLES, half]).start()
+        move(own_ref, me, half, sibling, sibsend.at[ROLES, half], sibrecv.at[ROLES, half]).start()
 
     def serve(role, half):
         slot = slots[role]
@@ -542,7 +589,7 @@
                         own_ref, slot, half, sibling, sibsend.at[role, half], sibrecv.at[role, half]
                     ).wait_send()
 
-    return begin, run, drain
+    return begin, serve, run, drain
 
 
 SENDS = 30
@@ -594,11 +641,11 @@
         pl.semaphore_signal(barrier, inc=1, device_id={"cp": peer}, device_id_type=MESH)
     pl.semaphore_wait(barrier, N_TP - 1 + len(around))
 
-    begin, run, drain = attention(
+    begin, serve, run, drain = attention(
         doc_ref, own, att, kv, qaug, logits, tops, best, acc, assem, arsem, sibsend, sibrecv
     )
     sent = projection(
-        h_ref, gain_ref, freq_ref, doc_ref, weights, inputs, qaug, own, begin,
+        h_ref, gain_ref, freq_ref, doc_ref, weights, inputs, qaug, own, begin, serve,
         gath, w, pacc, squares, cosine, sine, pssem, prsem, qssem, qrsem,
     )
     run()

time: 131 us -> 134 us (1.023)
  Pallas kernels: 128 us -> 130 us
    pallas_call x1, Pallas kernels: 128 us -> 130 us  [sublayer(): pl.pallas_call(fused_kernel, out_shape=jax.ShapeDtypeStruct((TOK, PIECE),...]
where the time goes in v5:
time: 134 us; the launch traced here: 133 us
  Pallas kernels  130 us (97%)
  local copies, waits for them, and re-layouts  3.21 us (2%)
    pallas_call x1, Pallas kernels, sublayer(): pl.pallas_call(fused_kernel, out_shape=jax.ShapeDtypeStruct((TOK, PIECE),...  130 us

profile of v5, /device:TPU:224, one launch (start us, length us, event | category | flops | bytes accessed | tf_op | source)
XLA Modules:
  0.0 133.1 jit_solution(13100908208095450212)
XLA Ops:
  0.0 1.3 %jit_solution_.3.freq_hbm = f32[64,128]{1,0:T(8,128)} broadcast(f32[64]{0:T(128)} %constant.2.clone), dimensions={0} | broadcast | bytes 33024 | tf_op jit(solution)
  1.3 129.9 %sublayer.1 = bf16[512,512]{1,0:T(8,128)(2,1)} custom-call(bf16[512,512]{1,0:T(8,128)(2,1)} %h_hbm.1, f32[1,4096]{1,0:T(1,128)} %bitcast.2, f32[64,128]{1,0:T(8,128)} %jit_solution_.3.freq_hbm, s32[1,512]{1,0:T(1,128)} %bitcast.3, bf16[4096,512]{1,0:T(8,128)(2,1)} %wq.1, bf16[4096,128]{1,0:T(8,128)(2,1)} %wk.1, bf16[4096,128]{1,0:T(8,128)(2,1)} %wv.1, ...), custom_call_target="tpu_custom_call" | custom-call | tf_op jit(solution)/shard_map/sublayer/pallas_call | solution.py:666
  131.2 1.9 %copy.10 = bf16[512,512]{1,0:T(8,128)(2,1)} copy(bf16[512,512]{1,0:T(8,128)(2,1)} %sublayer.1) | data formatting | bytes 1048576

commit v6 on v4

--- a/solution.py
+++ b/solution.py
@@ -2,7 +2,6 @@
 
 import jax
 import jax.numpy as jnp
-import numpy as np
 from jax import lax
 from jax.experimental import pallas as pl
 from jax.experimental.pallas import tpu as pltpu
@@ -52,7 +51,7 @@
 
 
 def projection(
-    h_ref, gain_ref, freq_ref, doc_ref, weights, inputs, q_out, kv_out, begin,
+    h_ref, gain_ref, doc_ref, weights, inputs, q_out, kv_out, begin,
     gath, w, acc, squares, cosine, sine, ssem, rsem, qssem, qrsem,
 ):
     t, up, down, far = tp_places()
@@ -113,7 +112,11 @@
 
     first = lax.axis_index("cp") * TOK
     place = (first + lax.broadcasted_iota(jnp.int32, (HEAD_SIZE // 2, TOK), 1)).astype(jnp.float32)
-    angle = place * jnp.concatenate([freq_ref[...]] * (TOK // 128), axis=1)
+    pair = lax.broadcasted_iota(jnp.int32, (HEAD_SIZE // 2, 128), 0)
+    freqs = jnp.zeros((HEAD_SIZE // 2, 128), jnp.float32)
+    for i in range(HEAD_SIZE // 2):
+        freqs = jnp.where(pair == i, jnp.float32(rope_base ** (-2.0 * i / HEAD_SIZE)), freqs)
+    angle = place * jnp.concatenate([freqs] * (TOK // 128), axis=1)
     cosine[...] = jnp.cos(angle)
     sine[...] = jnp.sin(angle)
     for peer in peers:
@@ -550,8 +553,8 @@
 
 
 def fused_kernel(
-    h_hbm, gain_hbm, freq_hbm, doc_hbm, wq, wk, wv, w_out, out_ref,
-    gath, w, pacc, squares, cosine, sine, gain_ref, freq_ref, doc_ref, insem, pssem, prsem, qssem, qrsem,
+    h_hbm, gain_hbm, doc_hbm, wq, wk, wv, w_out, out_ref,
+    gath, w, pacc, squares, cosine, sine, gain_ref, doc_ref, insem, pssem, prsem, qssem, qrsem,
     own, kv, qaug, logits, tops, best, acc, assem, arsem, sibsend, sibrecv, att,
     wo, terms, sums, across_in, side_in, half_in, side_end, across_end, wosem, cssem, crsem,
 ):
@@ -561,14 +564,13 @@
     h_ref = gath.at[t]
     inputs = [
         pltpu.make_async_copy(h_hbm, h_ref, insem.at[0]),
-        pltpu.make_async_copy(freq_hbm, freq_ref, insem.at[1]),
-        pltpu.make_async_copy(gain_hbm, gain_ref, insem.at[2]),
-        pltpu.make_async_copy(doc_hbm, doc_ref, insem.at[3]),
+        pltpu.make_async_copy(gain_hbm, gain_ref, insem.at[1]),
+        pltpu.make_async_copy(doc_hbm, doc_ref, insem.at[2]),
     ]
     weights = [
-        pltpu.make_async_copy(wq, w.at[:, 0:512], insem.at[4]),
-        pltpu.make_async_copy(wk, w.at[:, 512:640], insem.at[5]),
-        pltpu.make_async_copy(wv, w.at[:, 640:768], insem.at[6]),
+        pltpu.make_async_copy(wq, w.at[:, 0:512], insem.at[3]),
+        pltpu.make_async_copy(wk, w.at[:, 512:640], insem.at[4]),
+        pltpu.make_async_copy(wv, w.at[:, 640:768], insem.at[5]),
     ]
     order = [other(far), other(up), other(down), far, across, up, down, t]
     late = []
@@ -598,7 +600,7 @@
         doc_ref, own, att, kv, qaug, logits, tops, best, acc, assem, arsem, sibsend, sibrecv
     )
     sent = projection(
-        h_ref, gain_ref, freq_ref, doc_ref, weights, inputs, qaug, own, begin,
+        h_ref, gain_ref, doc_ref, weights, inputs, qaug, own, begin,
         gath, w, pacc, squares, cosine, sine, pssem, prsem, qssem, qrsem,
     )
     run()
@@ -612,14 +614,11 @@
 
 def sublayer(hidden, norm_gain, w_query, w_key, w_value, w_out, doc_ids):
     hbm = pl.BlockSpec(memory_space=pl.ANY)
-    powers = -np.arange(HEAD_SIZE // 2, dtype=np.float32) * np.float32(2.0) / HEAD_SIZE
-    freqs = (np.float64(rope_base) ** powers.astype(np.float64)).astype(np.float32)
-    freqs = jnp.asarray(np.broadcast_to(freqs[:, None], (HEAD_SIZE // 2, 128)))
     dma = pltpu.SemaphoreType.DMA
     return pl.pallas_call(
         fused_kernel,
         out_shape=jax.ShapeDtypeStruct((TOK, PIECE), BF16),
-        in_specs=[hbm] * 8,
+        in_specs=[hbm] * 7,
         out_specs=pl.BlockSpec(memory_space=pltpu.VMEM),
         scratch_shapes=[
             pltpu.VMEM((N_TP, TOK, PIECE), BF16),
@@ -629,9 +628,8 @@
             pltpu.VMEM((HEAD_SIZE // 2, TOK), F32),
             pltpu.VMEM((HEAD_SIZE // 2, TOK), F32),
             pltpu.VMEM((1, WIDTH), F32),
-            pltpu.VMEM((HEAD_SIZE // 2, 128), F32),
             pltpu.VMEM((1, TOK), jnp.int32),
-            dma((7,)),
+            dma((6,)),
             dma((28,)),
             dma((N_TP, CH)),
             dma((N_TP - 1,)),
@@ -665,7 +663,7 @@
         ),
         name="sublayer",
     )(
-        hidden, norm_gain.reshape(1, WIDTH), freqs, doc_ids.reshape(1, TOK),
+        hidden, norm_gain.reshape(1, WIDTH), doc_ids.reshape(1, TOK),
         w_query, w_key, w_value, w_out,
     )
 

time: 131 us -> 130 us (level)
  local copies, waits for them, and re-layouts: 3.21 us -> 1.87 us
    another operation x1 -> x0, local copies, waits for them, and re-layouts: 1.34 us -> none
where the time goes in v6:
time: 130 us
  Pallas kernels  128 us (98%)
  local copies, waits for them, and re-layouts  1.87 us (1%)
    pallas_call x1, Pallas kernels, sublayer(): pl.pallas_call(fused_kernel, out_shape=jax.ShapeDtypeStruct((TOK, PIECE),...  128 us

profile of v6, /device:TPU:224, one launch (start us, length us, event | category | flops | bytes accessed | tf_op | source)
XLA Modules:
  0.0 129.7 jit_solution(402620355934621776)
XLA Ops:
  0.0 127.8 %sublayer.1 = bf16[512,512]{1,0:T(8,128)(2,1)} custom-call(bf16[512,512]{1,0:T(8,128)(2,1)} %h_hbm.1, f32[1,4096]{1,0:T(1,128)} %bitcast.2, s32[1,512]{1,0:T(1,128)} %bitcast.3, bf16[4096,512]{1,0:T(8,128)(2,1)} %wq.1, bf16[4096,128]{1,0:T(8,128)(2,1)} %wk.1, bf16[4096,128]{1,0:T(8,128)(2,1)} %wv.1, bf16[512,4096]{1,0:T(8,128)(2,1)} %w_out.1), custom_call_target="tpu_custom_call" | custom-call | tf_op jit(solution)/shard_map/sublayer/pallas_call | solution.py:618
  127.8 1.9 %copy.9 = bf16[512,512]{1,0:T(8,128)(2,1)} copy(bf16[512,512]{1,0:T(8,128)(2,1)} %sublayer.1) | data formatting | bytes 1048576

commit v7 on v6

--- a/solution.py
+++ b/solution.py
@@ -442,8 +442,7 @@
         7: [(middle, left, (0, 1))],
         15: [(always, behind, (0, 1))],
         11: [(always, right, (0, 1)), (always, left, (1, 0))],
-        12: [(always, right, (0,))],
-        13: [(always, left, (1,))],
+        12: [(always, right, (0, 1))],
     }
     sends = []
 

time: 130 us -> 130 us (level)
  no operation moved by 1% of the time
where the time goes in v7:
time: 130 us
  Pallas kernels  128 us (98%)
  local copies, waits for them, and re-layouts  1.87 us (1%)
    pallas_call x1, Pallas kernels, sublayer(): pl.pallas_call(fused_kernel, out_shape=jax.ShapeDtypeStruct((TOK, PIECE),...  128 us

profile of v7, /device:TPU:224, one launch (start us, length us, event | category | flops | bytes accessed | tf_op | source)
XLA Modules:
  0.0 129.7 jit_solution(15251531368314542466)
XLA Ops:
  0.0 127.8 %sublayer.1 = bf16[512,512]{1,0:T(8,128)(2,1)} custom-call(bf16[512,512]{1,0:T(8,128)(2,1)} %h_hbm.1, f32[1,4096]{1,0:T(1,128)} %bitcast.2, s32[1,512]{1,0:T(1,128)} %bitcast.3, bf16[4096,512]{1,0:T(8,128)(2,1)} %wq.1, bf16[4096,128]{1,0:T(8,128)(2,1)} %wk.1, bf16[4096,128]{1,0:T(8,128)(2,1)} %wv.1, bf16[512,4096]{1,0:T(8,128)(2,1)} %w_out.1), custom_call_target="tpu_custom_call" | custom-call | tf_op jit(solution)/shard_map/sublayer/pallas_call | solution.py:617
  127.8 1.9 %copy.9 = bf16[512,512]{1,0:T(8,128)(2,1)} copy(bf16[512,512]{1,0:T(8,128)(2,1)} %sublayer.1) | data formatting | bytes 1048576
